TPU v7x, 32 devices: a whole 2x2x4 slice. The times are simulated.
32 devices in a mesh: pop: 8 (over z, y), mp: 4 (over x, core).
Axes of the slice: x: 2, y: 2, z: 4, core: 2. Of those that a mesh axis runs over, the one named last changes fastest.
Arguments:
- token_ids: int32 [96, 4, 16], P('pop'), may hold values from 0 to 255
- fitness_ranks: int32 [96], P('pop'), may hold values from 0 to 143, as said below
- embedding: bfloat16 [256, 4096], P(None, 'mp'), may hold values from -6 to 6
- mix_weights: bfloat16 [2, 4096, 4096], P(None, 'mp'), may hold values from -0.09375 to 0.09375
- factors_in: bfloat16 [2, 96, 4, 4096], P(None, 'pop', None, 'mp'), may hold values from -6 to 6
- factors_out: bfloat16 [2, 96, 4, 4096], P(None, 'pop'), may hold values from -6 to 6
- decay_rates: float32 [2, 4096], P(None, 'mp'), may hold values from 0.2 to 0.98
- norm_gain: float32 [2, 4096], P(None, 'mp'), may hold values from 0.1 to 1.9
- reward_dir: float32 [4096], P('mp'), may hold values from -6 to 6
Outputs:
- final_features: bfloat16 [96, 4, 4096], P('pop', None, 'mp')
- scores: float32 [96, 4], P('pop')
- weight_step: float32 [2, 4096, 4096], P(None, 'mp', 'pop')
Inputs may be any that keep to these rules, and one draw needn't show every extreme that they name: `fitness_ranks`: ranks may repeat.
All inputs are finite; a program needn't handle non-finite values.
Results may differ from a plain program's by a relative error of at most 0.023.
Values may be sent and summed in bfloat16 or wider, within the bound.
A program may use at most 128 MiB of HBM per device.

v0:
```python
import jax
import jax.numpy as jnp
from jax import lax
from jax.sharding import PartitionSpec as P

noise_scale = 0.25
norm_eps = 1e-06
spread_eps = 1e-05


def recurrence(inputs, decay):
    time_major = jnp.moveaxis(inputs, 2, 0)

    def advance(carried, column):
        carried = decay * carried + (1.0 - decay) * column
        return (carried, carried)

    initial = jnp.zeros(time_major.shape[1:], jnp.float32)
    _, states = lax.scan(advance, initial, time_major)
    return jnp.moveaxis(states, 0, 2)


def mixed_inputs(hidden, weight_rows):
    flat = hidden.reshape(-1, hidden.shape[3])
    partial_value = jnp.dot(flat, weight_rows, preferred_element_type=jnp.float32)
    summed = lax.psum_scatter(
        partial_value.astype(jnp.bfloat16), "mp", scatter_dimension=1, tiled=True
    ).astype(jnp.float32)
    return summed.reshape(hidden.shape)


def project_rank(hidden, factor_rows):
    return jnp.einsum("mstd,mrd->mstr", hidden, factor_rows, preferred_element_type=jnp.float32)


def shards(
    token_ids,
    fitness_ranks,
    embedding,
    mix_weights,
    factors_in,
    factors_out,
    decay_rates,
    norm_gain,
    reward_dir,
):
    members, seq_count, step_count = token_ids.shape
    local_width = embedding.shape[1]
    vocab_size = embedding.shape[0]
    layers = mix_weights.shape[0]
    full_width = mix_weights.shape[2]
    rank_count = factors_in.shape[2]
    pop_count = lax.axis_size("pop")
    members_all = members * pop_count
    coef = noise_scale * (full_width * rank_count) ** (-0.5)
    position = lax.axis_index("mp")
    outputs_local = lax.dynamic_slice_in_dim(
        factors_out, position * local_width, local_width, 3
    ).astype(jnp.float32)
    onehot = (
        token_ids.reshape(-1)[:, None] == jnp.arange(vocab_size, dtype=jnp.int32)[None, :]
    ).astype(jnp.bfloat16)
    hidden = jnp.dot(onehot, embedding, preferred_element_type=jnp.float32).astype(jnp.bfloat16)
    hidden = hidden.reshape(members, seq_count, step_count, local_width)
    for layer_idx in range(layers):
        base_mix = mixed_inputs(hidden, mix_weights[layer_idx])
        low_rank = lax.psum(project_rank(hidden, factors_in[layer_idx]), "mp")
        correction = jnp.einsum(
            "mstr,mrd->mstd", low_rank, outputs_local[layer_idx], precision=lax.Precision.HIGHEST
        )
        states = recurrence(base_mix + coef * correction, decay_rates[layer_idx])
        squares = lax.psum(jnp.sum(states * states, axis=3), "mp")
        norm_scale = lax.rsqrt(squares / full_width + norm_eps)
        hidden = (
            hidden.astype(jnp.float32) + states * norm_scale[..., None] * norm_gain[layer_idx]
        ).astype(jnp.bfloat16)
    dots_local = jnp.einsum(
        "mstd,d->mst", hidden.astype(jnp.float32), reward_dir, precision=lax.Precision.HIGHEST
    )
    reward_terms = lax.psum(dots_local, "mp")
    final_features = hidden[:, :, step_count - 1, :]
    scores = jnp.mean(reward_terms, axis=2) * full_width ** (-0.5)
    ranks_every = lax.all_gather(fitness_ranks, "pop", axis=0, tiled=True)
    shares_all = ranks_every.astype(jnp.float32) / members_all
    rank_mean = jnp.mean(shares_all)
    rank_spread = jnp.mean((shares_all - rank_mean) * (shares_all - rank_mean)) + spread_eps
    shaped_all = (shares_all - rank_mean) * lax.rsqrt(rank_spread)
    columns = lax.all_to_all(factors_out, "pop", split_axis=3, concat_axis=1, tiled=True)
    weighted = (
        lax.all_gather(factors_in, "pop", axis=1, tiled=True).astype(jnp.float32)
        * shaped_all[None, :, None, None]
    ).astype(jnp.bfloat16)
    weight_delta = jnp.einsum(
        "lmri,lmro->lio", weighted, columns, preferred_element_type=jnp.float32
    )
    weight_step = weight_delta * (members_all * rank_count) ** (-0.5)
    return (final_features, scores, weight_step)


def solution(mesh):
    return jax.shard_map(
        shards,
        mesh=mesh,
        in_specs=(
            P("pop", None, None),
            P("pop"),
            P(None, "mp"),
            P(None, "mp", None),
            P(None, "pop", None, "mp"),
            P(None, "pop", None, None),
            P(None, "mp"),
            P(None, "mp"),
            P("mp"),
        ),
        out_specs=(P("pop", None, "mp"), P("pop", None), P(None, "mp", "pop")),
        check_vma=False,
    )
```

profile of v0, /device:TPU:0, one launch (start us, length us, event | category | flops | bytes accessed | tf_op | source)
XLA Modules:
  0.0 486.0 jit_solution(6501200534293867005)
XLA Ops:
  9.7 12.5 %fusion.10 = bf16[768,4096]{1,0:T(8,128)(2,1)} fusion(bf16[768,1024]{1,0:T(8,128)(2,1)S(1)} %convolution_convert_fusion, bf16[2,1024,4096]{2,1,0:T(8,128)(2,1)} %param.16), kind=kOutput, calls=%fused_computation.18 | convolution fusion | flops 6445596672 | bytes 16252928 | tf_op jit(solution)/shard_map/dot_general | solution.py:25
  25.1 13.9 %psum.35 = f32[12,4,16,4]{2,3,1,0:T(4,128)S(1)} all-reduce(f32[12,4,16,4]{2,3,1,0:T(4,128)S(1)} %fusion.31), channel_id=1, replica_groups=mesh['pop'=8,'mp'=4] {'mp'}, use_global_device_ids=true, to_apply=%region_1.0 | all-reduce | flops 3072 | bytes 24576 | tf_op jit(solution)/shard_map/psum | solution.py:67
  39.1 43.9 %reduce-scatter.3.cloned.1.call-done = bf16[768,1024]{1,0:T(8,128)(2,1)} async-done(((bf16[768,4096]{1,0:T(8,128)(2,1)}), bf16[768,1024]{1,0:T(8,128)(2,1)}) %reduce-scatter.3.cloned.1.call-update) | async-done | bytes 1572880 | tf_op jit(solution)/shard_map/reduce_scatter | solution.py:26
  89.2 108.1 %while.26 = (s32[]{:T(128)}, f32[12,4,1024]{2,1,0:T(4,128)S(1)}, f32[16,12,4,1024]{3,0,2,1:T(8,128)}, f32[1,1024]{1,0:T(1,128)S(1)}, f32[1024]{0:T(1024)S(1)}, /...) while((s32[]{:T(128)}, f32[12,4,1024]{2,1,0:T(4,128)S(1)}, f32[16,12,4,1024]{3,0,2,1:T(8,128)}, ...), condition=%wide.region_3.4_spmd.clone, body=%wide.region_2.3_spmd.clone.sunk | while | flops 197635 | bytes 1785959 | solution.py:19
  91.1 4.8 dynamic_update_slice.11
  97.9 4.8 dynamic_update_slice.11
  104.6 4.8 dynamic_update_slice.11
  111.4 4.8 dynamic_update_slice.11
  118.1 4.8 dynamic_update_slice.11
  124.9 4.8 dynamic_update_slice.11
  131.6 4.8 dynamic_update_slice.11
  138.4 4.8 dynamic_update_slice.11
  145.2 4.8 dynamic_update_slice.11
  151.9 4.8 dynamic_update_slice.11
  158.7 4.8 dynamic_update_slice.11
  165.4 4.8 dynamic_update_slice.11
  172.2 4.8 dynamic_update_slice.11
  178.9 4.8 dynamic_update_slice.11
  185.7 4.8 dynamic_update_slice.11
  192.4 4.8 dynamic_update_slice.11
  199.4 10.4 %psum.36 = f32[12,4,16]{2,1,0:T(4,128)S(1)} all-reduce(f32[12,4,16]{2,1,0:T(4,128)S(1)} %fusion.22), channel_id=1, replica_groups=mesh['pop'=8,'mp'=4] {'mp'}, use_global_device_ids=true, to_apply=%region_5.6 | all-reduce | flops 768 | bytes 6144 | tf_op jit(solution)/shard_map/psum | solution.py:72
  212.8 12.0 %fusion.13 = bf16[768,4096]{1,0:T(8,128)(2,1)} fusion(bf16[768,1024]{1,0:T(8,128)(2,1)S(1)} %bitcast.129, bf16[2,1024,4096]{2,1,0:T(8,128)(2,1)} %param.16), kind=kOutput, calls=%fused_computation.19 | convolution fusion | flops 6445596672 | bytes 16252928 | tf_op jit(solution)/shard_map/dot_general | solution.py:25
  224.8 9.1 %copy.51 = bf16[2,12,4,4096]{1,2,0,3:T(4,128)(2,1)} copy(bf16[2,12,4,4096]{3,2,1,0:T(4,128)(2,1)S(1)} %copy-done.3) | data formatting | bytes 1572864 | tf_op args[5]
  233.9 17.6 %reshape.60 = bf16[8,2,24576]{2,1,0:T(2,128)(2,1)} reshape(bf16[4096,2,4,12]{3,2,1,0:T(4,128)(2,1)} %bitcast.126) | data formatting | bytes 1572864
  251.6 5.6 %all-to-all-start = ((bf16[8,2,24576]{2,1,0:T(2,128)(2,1)}), bf16[8,2,24576]{2,1,0:T(2,128)(2,1)S(1)}, u32[]{:S(2)}, u32[]{:S(2)}) async-start(bf16[8,2,24576]{2,1,0:T(2,128)(2,1)} %reshape.60), calls=%async_computation.2 | async-start | bytes 1572864 | tf_op jit(solution)/shard_map/all_to_all | solution.py:88
  258.7 18.6 %all-reduce = s32[96]{0:T(128)S(1)} all-reduce(s32[96]{0:T(128)S(1)} %dynamic-update-slice), channel_id=1, replica_groups=mesh['pop'=8,'mp'=4] {'pop'}, use_global_device_ids=true, to_apply=%add | all-reduce | flops 96 | bytes 768
  279.8 20.4 %reshape.61 = bf16[4096,2,4,12]{3,2,1,0:T(4,128)(2,1)} reshape(bf16[8,2,24576]{2,1,0:T(2,128)(2,1)S(1)} %all-to-all-done) | data formatting | bytes 1572864
  300.2 12.0 %copy.52 = bf16[2,12,4,8,512]{4,2,1,3,0:T(4,128)(2,1)S(1)} copy(bf16[2,12,4,8,512]{1,2,0,4,3:T(4,128)(2,1)} %bitcast.125) | data formatting | bytes 1572864 | tf_op jit(solution)/shard_map/all_to_all | solution.py:88
  319.7 11.3 %psum.37 = f32[12,4,16,4]{2,3,1,0:T(4,128)S(1)} all-reduce(f32[12,4,16,4]{2,3,1,0:T(4,128)S(1)} %fusion.29), channel_id=1, replica_groups=mesh['pop'=8,'mp'=4] {'mp'}, use_global_device_ids=true, to_apply=%region_7.8 | all-reduce | flops 3072 | bytes 24576 | tf_op jit(solution)/shard_map/psum | solution.py:67
  337.3 108.2 %while.27 = (s32[]{:T(128)}, f32[12,4,1024]{2,1,0:T(4,128)S(1)}, f32[16,12,4,1024]{3,0,2,1:T(8,128)}, f32[1,1024]{1,0:T(1,128)S(1)}, f32[1024]{0:T(1024)S(1)}, /...) while((s32[]{:T(128)}, f32[12,4,1024]{2,1,0:T(4,128)S(1)}, f32[16,12,4,1024]{3,0,2,1:T(8,128)}, ...), condition=%wide.region_9.10_spmd.clone, body=%wide.region_8.9_spmd.clone.sunk | while | flops 197635 | bytes 1785959 | solution.py:19
  339.2 4.8 dynamic_update_slice.12
  346.0 4.8 dynamic_update_slice.12
  352.7 4.8 dynamic_update_slice.12
  359.5 4.8 dynamic_update_slice.12
  366.2 4.8 dynamic_update_slice.12
  373.0 4.8 dynamic_update_slice.12
  379.7 4.8 dynamic_update_slice.12
  393.2 4.9 dynamic_update_slice.12
  400.0 4.9 dynamic_update_slice.12
  406.8 4.9 dynamic_update_slice.12
  413.5 4.9 dynamic_update_slice.12
  420.3 4.9 dynamic_update_slice.12
  427.1 4.9 dynamic_update_slice.12
  433.9 4.9 dynamic_update_slice.12
  440.7 4.9 dynamic_update_slice.12
  447.7 10.4 %psum.38 = f32[12,4,16]{2,1,0:T(4,128)S(1)} all-reduce(f32[12,4,16]{2,1,0:T(4,128)S(1)} %fusion.18), channel_id=1, replica_groups=mesh['pop'=8,'mp'=4] {'mp'}, use_global_device_ids=true, to_apply=%region_11.12 | all-reduce | flops 768 | bytes 6144 | tf_op jit(solution)/shard_map/psum | solution.py:72
  461.6 5.6 %fusion.41 = f32[1,12,4,16]{3,0,2,1:T(1,128)S(1)} fusion(bf16[12,4,16,1024]{3,2,1,0:T(8,128)(2,1)S(1)} %fusion.21, f32[1024,1,1,1]{0,1,3,2:T(1,128)S(1)} %bitcast.143), kind=kOutput, calls=%fused_computation.64 | convolution fusion | flops 9437184 | bytes 1580032 | tf_op jit(solution)/shard_map/mstd,d->mst/dot_general | solution.py:77
  467.1 10.6 %psum.39 = f32[12,4,16]{2,1,0:T(4,128)S(1)} all-reduce(f32[12,4,16]{2,1,0:T(4,128)S(1)} %bitcast.140), channel_id=1, replica_groups=mesh['pop'=8,'mp'=4] {'mp'}, use_global_device_ids=true, to_apply=%region_12.13 | all-reduce | flops 768 | bytes 6144 | tf_op jit(solution)/shard_map/psum | solution.py:80
  (189 shorter events, 103.4 us)
Async XLA Ops:
  8.0 1.1 copy-start
  8.0 75.0 %reduce-scatter.3.cloned.1.call-start = ((), (), s32[]{:S(2)}) async-start(), calls=%async_computation.3 | async-start | bytes 7864320 | tf_op jit(solution)/shard_map/reduce_scatter | solution.py:26
  9.7 13.2 %copy-start.2 = (bf16[768,1024]{1,0:T(8,128)(2,1)}, bf16[768,1024]{1,0:T(8,128)(2,1)S(1)}, u32[]{:S(2)}) copy-start(bf16[768,1024]{1,0:T(8,128)(2,1)S(1)} %convolution_convert_fusion) | copy-start | bytes 4718596
  22.2 0.9 copy-start.4
  22.2 16.8 %copy-start.5 = (f32[2,1024]{1,0:T(2,128)S(1)}, f32[2,1024]{1,0:T(2,128)}, u32[]{:S(2)}) copy-start(f32[2,1024]{1,0:T(2,128)} %param.19) | copy-start | bytes 24580
  22.2 16.8 %copy-start.6 = (f32[2,1024]{1,0:T(2,128)S(1)}, f32[2,1024]{1,0:T(2,128)}, u32[]{:S(2)}) copy-start(f32[2,1024]{1,0:T(2,128)} %param.20) | copy-start | bytes 24580
  22.2 60.8 %copy-start.3 = (bf16[2,12,4,4096]{3,2,1,0:T(4,128)(2,1)S(1)}, bf16[2,12,4,4096]{3,2,1,0:T(4,128)(2,1)}, u32[]{:S(2)}) copy-start(bf16[2,12,4,4096]{3,2,1,0:T(4,128)(2,1)} %param.18) | copy-start | bytes 2359300
  22.2 290.0 %all-gather.2.cloned.1.call-start = ((), (), s32[]{:S(2)}) async-start(), calls=%async_computation.5 | async-start | bytes 1769472 | tf_op jit(solution)/shard_map/all_gather | solution.py:90
  22.8 308.2 %reduce-scatter.5.cloned.1.call-start = ((), (), s32[]{:S(2)}) async-start(), calls=%async_computation.4 | async-start | bytes 7864320 | tf_op jit(solution)/shard_map/reduce_scatter | solution.py:26
  233.9 23.2 %copy-start.9 = (u32[32]{0:T(128)S(1)}, u32[32]{0:T(128)}, u32[]{:S(2)}) copy-start(u32[32]{0:T(128)} %constant.63) | copy-start | bytes 388
  233.9 24.5 %copy-start.8 = (s32[12]{0:T(128)S(1)}, s32[12]{0:T(128)}, u32[]{:S(2)}) copy-start(s32[12]{0:T(128)} %param.14) | copy-start | bytes 148
  251.6 28.2 %all-to-all-start = ((bf16[8,2,24576]{2,1,0:T(2,128)(2,1)}), bf16[8,2,24576]{2,1,0:T(2,128)(2,1)S(1)}, u32[]{:S(2)}, u32[]{:S(2)}) async-start(bf16[8,2,24576]{2,1,0:T(2,128)(2,1)} %reshape.60), calls=%async_computation.2 | async-start | bytes 1572864 | tf_op jit(solution)/shard_map/all_to_all | solution.py:88
  458.1 20.4 %copy-start.1 = (bf16[256,1024]{1,0:T(8,128)(2,1)S(1)}, bf16[256,1024]{1,0:T(8,128)(2,1)}, u32[]{:S(2)}) copy-start(bf16[256,1024]{1,0:T(8,128)(2,1)} %param.15) | copy-start | bytes 1572868
  458.1 3.4 copy-start.7
Sparse Core Ops, SparseCore 0:
  22.4 60.5 reduce-scatter.2
  224.9 58.2 reduce-scatter.4
Sparse Core Ops, SparseCore 1:
  24.9 46.8 all-gather.1
where the time goes:
time: 491 us; the launch traced here: 486 us
  local copies, waits for them, and re-layouts  278 us (57%)
  blocking collectives  75.3 us (15%)
  matrix products  46.3 us (9%)
  waiting for transfers between devices  44.5 us (9%)
  between operations  17.7 us (4%)
  other arithmetic  17 us (3%)
  starting transfers between devices  5.72 us (1%)
    dynamic_update_slice x64, local copies, waits for them, and re-layouts, recurrence(): _, states = lax.scan(advance, initial, time_major)  161 us
    dynamic_slice x32, local copies, waits for them, and re-layouts, recurrence(): _, states = lax.scan(advance, initial, time_major)  50.3 us
    unnamed x28, local copies, waits for them, and re-layouts  49.7 us
    reduce_scatter x2, waiting for transfers between devices, mixed_inputs(): lax.psum_scatter(partial_value.astype(jnp.bfloat16), 'mp', scatter_dimens...  44 us
    psum x2, blocking collectives, shards(): low_rank = lax.psum(project_rank(hidden, factors_in[layer_idx]), 'mp')  25.2 us
    dot_general x2, matrix products, mixed_inputs(): jnp.dot(flat, weight_rows, preferred_element_type=jnp.float32)  24.5 us
    psum x2, blocking collectives, shards(): squares = lax.psum(jnp.sum(states * states, axis=3), 'mp')  20.9 us
    unnamed x1, blocking collectives  18.6 us
  transfers between devices with their start and end apart: 4, of which 1 were waited for; matrix products, arithmetic and copies ran while one was open for 41% of the time, Pallas kernels for 0%

commit v1 on v0

--- a/solution.py
+++ b/solution.py
@@ -9,28 +9,25 @@
 
 
 def recurrence(inputs, decay):
-    time_major = jnp.moveaxis(inputs, 2, 0)
-
-    def advance(carried, column):
-        carried = decay * carried + (1.0 - decay) * column
-        return (carried, carried)
-
-    initial = jnp.zeros(time_major.shape[1:], jnp.float32)
-    _, states = lax.scan(advance, initial, time_major)
-    return jnp.moveaxis(states, 0, 2)
+    carried = jnp.zeros(inputs.shape[1:], jnp.float32)
+    states = []
+    for step in range(inputs.shape[0]):
+        carried = decay * carried + (1.0 - decay) * inputs[step]
+        states.append(carried)
+    return jnp.stack(states, axis=0)
 
 
 def mixed_inputs(hidden, weight_rows):
-    flat = hidden.reshape(-1, hidden.shape[3])
+    flat = hidden.reshape(-1, hidden.shape[-1])
     partial_value = jnp.dot(flat, weight_rows, preferred_element_type=jnp.float32)
     summed = lax.psum_scatter(
         partial_value.astype(jnp.bfloat16), "mp", scatter_dimension=1, tiled=True
     ).astype(jnp.float32)
-    return summed.reshape(hidden.shape)
+    return summed
 
 
 def project_rank(hidden, factor_rows):
-    return jnp.einsum("mstd,mrd->mstr", hidden, factor_rows, preferred_element_type=jnp.float32)
+    return jnp.einsum("tmsd,mrd->tmsr", hidden, factor_rows, preferred_element_type=jnp.float32)
 
 
 def shards(
@@ -58,15 +55,24 @@
         factors_out, position * local_width, local_width, 3
     ).astype(jnp.float32)
     onehot = (
-        token_ids.reshape(-1)[:, None] == jnp.arange(vocab_size, dtype=jnp.int32)[None, :]
+        jnp.moveaxis(token_ids, 2, 0).reshape(-1)[:, None] == jnp.arange(vocab_size, dtype=jnp.int32)[None, :]
     ).astype(jnp.bfloat16)
     hidden = jnp.dot(onehot, embedding, preferred_element_type=jnp.float32).astype(jnp.bfloat16)
-    hidden = hidden.reshape(members, seq_count, step_count, local_width)
+    hidden = hidden.reshape(step_count, members, seq_count, local_width)
     for layer_idx in range(layers):
-        base_mix = mixed_inputs(hidden, mix_weights[layer_idx])
+        if layer_idx == 0:
+            table = mixed_inputs(embedding, mix_weights[0])
+            top = table.astype(jnp.bfloat16)
+            rest = (table - top.astype(jnp.float32)).astype(jnp.bfloat16)
+            base_mix = jnp.dot(onehot, top, preferred_element_type=jnp.float32) + jnp.dot(
+                onehot, rest, preferred_element_type=jnp.float32
+            )
+        else:
+            base_mix = mixed_inputs(hidden, mix_weights[layer_idx])
+        base_mix = base_mix.reshape(hidden.shape)
         low_rank = lax.psum(project_rank(hidden, factors_in[layer_idx]), "mp")
         correction = jnp.einsum(
-            "mstr,mrd->mstd", low_rank, outputs_local[layer_idx], precision=lax.Precision.HIGHEST
+            "tmsr,mrd->tmsd", low_rank, outputs_local[layer_idx], precision=lax.Precision.HIGHEST
         )
         states = recurrence(base_mix + coef * correction, decay_rates[layer_idx])
         squares = lax.psum(jnp.sum(states * states, axis=3), "mp")
@@ -75,11 +81,11 @@
             hidden.astype(jnp.float32) + states * norm_scale[..., None] * norm_gain[layer_idx]
         ).astype(jnp.bfloat16)
     dots_local = jnp.einsum(
-        "mstd,d->mst", hidden.astype(jnp.float32), reward_dir, precision=lax.Precision.HIGHEST
+        "tmsd,d->tms", hidden.astype(jnp.float32), reward_dir, precision=lax.Precision.HIGHEST
     )
     reward_terms = lax.psum(dots_local, "mp")
-    final_features = hidden[:, :, step_count - 1, :]
-    scores = jnp.mean(reward_terms, axis=2) * full_width ** (-0.5)
+    final_features = hidden[step_count - 1]
+    scores = jnp.mean(reward_terms, axis=0) * full_width ** (-0.5)
     ranks_every = lax.all_gather(fitness_ranks, "pop", axis=0, tiled=True)
     shares_all = ranks_every.astype(jnp.float32) / members_all
     rank_mean = jnp.mean(shares_all)

time: 491 us -> 308 us (0.63)
  local copies, waits for them, and re-layouts: 278 us -> 82.4 us
  other arithmetic: 17 us -> 64.7 us
  waiting for transfers between devices: 44.5 us -> 10.2 us
    dynamic_update_slice x64 -> x0, local copies, waits for them, and re-layouts: 161 us -> none  [recurrence(): _, states = lax.scan(advance, initial, time_major)]
    dynamic_slice x32 -> x0, local copies, waits for them, and re-layouts: 50.3 us -> none  [recurrence(): _, states = lax.scan(advance, initial, time_major)]
    unnamed x2 -> x30, other arithmetic: 0.01 us -> 38.4 us
    reduce_scatter x2, waiting for transfers between devices: 44 us -> 9.64 us  [mixed_inputs(): lax.psum_scatter(partial_value.astype(jnp.bfloat16), 'mp', scatter_dimens...]
    reshape x0 -> x3, local copies, waits for them, and re-layouts: none -> 11 us  [the longest x2 8.94 us: shards(): base_mix = base_mix.reshape(hidden.shape)]
    add x32 -> x2, other arithmetic: 3.76 us -> 10.6 us  [shards(): states = recurrence(base_mix + coef * correction, decay_rates[layer_idx])]
    unnamed x28 -> x39, local copies, waits for them, and re-layouts: 49.7 us -> 53.2 us
    dot_general x5 -> x7, matrix products: 17.7 us -> 21.1 us  [the longest x2 6.23 us: shards(): jnp.einsum('tmsr,mrd->tmsd', low_rank, outputs_local[layer_idx], precisio...]
  transfers between devices with their start and end apart: 4 -> 4, of which waited for: 1 -> 1; matrix products, arithmetic and copies ran while one was open for 41% -> 48% of each run, Pallas kernels for 0% -> 0%
where the time goes in v1:
time: 308 us; the launch traced here: 303 us
  local copies, waits for them, and re-layouts  82.4 us (27%)
  blocking collectives  76.7 us (25%)
  other arithmetic  64.7 us (21%)
  matrix products  45 us (15%)
  between operations  18.2 us (6%)
  waiting for transfers between devices  10.2 us (3%)
  starting transfers between devices  5.86 us (2%)
    unnamed x39, local copies, waits for them, and re-layouts  53.2 us
    unnamed x30, other arithmetic  38.4 us
    psum x2, blocking collectives, shards(): low_rank = lax.psum(project_rank(hidden, factors_in[layer_idx]), 'mp')  26.1 us
    psum x2, blocking collectives, shards(): squares = lax.psum(jnp.sum(states * states, axis=3), 'mp')  21.5 us
    dot_general x2, matrix products, mixed_inputs(): jnp.dot(flat, weight_rows, preferred_element_type=jnp.float32)  19.8 us
    unnamed x1, blocking collectives  18.6 us
    all_to_all x1, local copies, waits for them, and re-layouts, shards(): lax.all_to_all(factors_out, 'pop', split_axis=3, concat_axis=1, tiled=True)  12 us
    add x2, other arithmetic, shards(): states = recurrence(base_mix + coef * correction, decay_rates[layer_idx])  10.6 us
  transfers between devices with their start and end apart: 4, of which 1 were waited for; matrix products, arithmetic and copies ran while one was open for 48% of the time, Pallas kernels for 0%

profile of v1, /device:TPU:0, one launch (start us, length us, event | category | flops | bytes accessed | tf_op | source)
XLA Modules:
  0.0 303.0 jit_solution(9531522630871206582)
XLA Ops:
  9.0 7.0 %fusion.9 = bf16[256,4096]{1,0:T(8,128)(2,1)} fusion(bf16[256,1024]{1,0:T(8,128)(2,1)S(1)} %copy-done, bf16[2,1024,4096]{2,1,0:T(8,128)(2,1)} %param.12), kind=kOutput, calls=%fused_computation.7 | convolution fusion | flops 2148532224 | bytes 11010048 | tf_op jit(solution)/shard_map/dot_general | solution.py:22
  17.7 2.0 reshape.39
  19.8 3.4 %fusion.23 = f32[16,12,4,4]{0,3,2,1:T(4,128)S(1)} fusion(bf16[16,12,4,1024]{3,2,1,0:T(4,128)(2,1)} %reshape.39, bf16[2,12,4,1024]{3,2,1,0:T(4,128)(2,1)S(1)} %copy-done.8), kind=kOutput, calls=%fused_computation.32 | convolution fusion | flops 6291456 | bytes 1683456 | tf_op jit(solution)/shard_map/tmsd,mrd->tmsr/dot_general | solution.py:30
  23.1 14.3 %psum.35 = f32[16,12,4,4]{0,3,2,1:T(4,128)S(1)} all-reduce(f32[16,12,4,4]{0,3,2,1:T(4,128)S(1)} %fusion.23), channel_id=1, replica_groups=mesh['pop'=8,'mp'=4] {'mp'}, use_global_device_ids=true, to_apply=%region_1.0 | all-reduce | flops 3072 | bytes 24576 | tf_op jit(solution)/shard_map/psum | solution.py:73
  37.4 3.1 %convolution_multiply_fusion.1 = f32[12,1024,16,4]{1,2,3,0:T(8,128)} fusion(f32[16,12,4,4]{0,3,2,1:T(4,128)S(1)} %psum.35, bf16[2,12,4,4096]{3,2,1,0:T(4,128)(2,1)S(1)} %copy-done.7, s32[]{:T(128)S(6)} %select_n.3), kind=kOutput, calls=%fused_computation.21 | convolution fusion | flops 38535168 | bytes 3342340 | tf_op jit(solution)/shard_map/tmsr,mrd->tmsd/dot_general | solution.py:74
  40.5 9.6 %reduce-scatter.3.cloned.1.call-done = bf16[256,1024]{1,0:T(8,128)(2,1)} async-done(((bf16[256,4096]{1,0:T(8,128)(2,1)}), bf16[256,1024]{1,0:T(8,128)(2,1)}) %reduce-scatter.3.cloned.1.call-update) | async-done | bytes 524304 | tf_op jit(solution)/shard_map/reduce_scatter | solution.py:23
  50.2 1.7 fusion.30
  51.9 2.3 convolution_add_fusion
  54.2 4.8 %reshape.40 = f32[16,12,4,1024]{3,2,1,0:T(4,128)} reshape(f32[768,1024]{1,0:T(8,128)} %convolution_add_fusion) | data formatting | bytes 6291456 | tf_op jit(solution)/shard_map/reshape | solution.py:72
  59.0 5.3 %fusion.13 = f32[16,12,4,1024]{3,2,1,0:T(4,128)S(1)} fusion(f32[16,12,4,1024]{3,2,1,0:T(4,128)} %reshape.40, f32[12,1024,16,4]{1,2,3,0:T(8,128)} %convolution_multiply_fusion.1), kind=kLoop, calls=%fused_computation.12 | loop fusion | flops 786432 | bytes 9437184 | tf_op jit(solution)/shard_map/add | solution.py:77
  66.1 1.7 constant_dynamic-update-slice_fusion.12
  67.8 1.8 constant_dynamic-update-slice_fusion.11
  69.6 1.7 constant_dynamic-update-slice_fusion.10
  71.3 1.8 constant_dynamic-update-slice_fusion.9
  73.1 1.7 constant_dynamic-update-slice_fusion.8
  74.7 1.8 constant_dynamic-update-slice_fusion.7
  76.5 1.7 constant_dynamic-update-slice_fusion.6
  78.2 1.8 constant_dynamic-update-slice_fusion.5
  80.0 1.7 constant_dynamic-update-slice_fusion.4
  81.7 1.8 constant_dynamic-update-slice_fusion.3
  83.5 1.7 constant_dynamic-update-slice_fusion.2
  85.2 1.8 constant_dynamic-update-slice_fusion.1
  87.0 1.7 constant_dynamic-update-slice_fusion
  88.6 1.8 fusion.52
  90.4 4.9 %stack.7 = f32[768,1024]{1,0:T(8,128)} reshape(f32[16,12,4,1024]{3,2,1,0:T(4,128)} %fusion.52) | data formatting | bytes 6291456 | tf_op jit(solution)/shard_map/stack | solution.py:17
  95.3 2.6 multiply_reduce_fusion.1
  98.1 10.9 %psum.36 = f32[16,12,4]{0,2,1:T(4,128)S(1)} all-reduce(f32[16,12,4]{0,2,1:T(4,128)S(1)} %copy.84), channel_id=1, replica_groups=mesh['pop'=8,'mp'=4] {'mp'}, use_global_device_ids=true, to_apply=%region_3.0 | all-reduce | flops 768 | bytes 6144 | tf_op jit(solution)/shard_map/psum | solution.py:78
  109.3 12.7 %fusion.6 = bf16[768,4096]{1,0:T(8,128)(2,1)} fusion(bf16[2,1024,4096]{2,1,0:T(8,128)(2,1)} %param.12, f32[768,1024]{1,0:T(8,128)} %stack.7, bf16[768,1024]{1,0:T(8,128)(2,1)S(1)} %convolution_convert_fusion, f32[1024]{0:T(1024)S(1)} %bitcast.112, f32[768]{0:T(1024)S(1)} %mul.1061), kind=kOutput, calls=%fused_computation.6 | convolution fusion | flops 6449528832 | bytes 19405824 | tf_op jit(solution)/shard_map/dot_general | solution.py:22
  122.0 9.1 %copy.71 = bf16[2,12,4,4096]{1,2,0,3:T(4,128)(2,1)} copy(bf16[2,12,4,4096]{3,2,1,0:T(4,128)(2,1)S(1)} %copy-done.7) | data formatting | bytes 1572864 | tf_op args[5]
  131.2 17.7 %reshape.57 = bf16[8,2,24576]{2,1,0:T(2,128)(2,1)} reshape(bf16[4096,2,4,12]{3,2,1,0:T(4,128)(2,1)} %bitcast.75) | data formatting | bytes 1572864
  148.9 5.7 %all-to-all-start = ((bf16[8,2,24576]{2,1,0:T(2,128)(2,1)}), bf16[8,2,24576]{2,1,0:T(2,128)(2,1)S(1)}, u32[]{:S(2)}, u32[]{:S(2)}) async-start(bf16[8,2,24576]{2,1,0:T(2,128)(2,1)} %reshape.57), calls=%async_computation.2 | async-start | bytes 1572864 | tf_op jit(solution)/shard_map/all_to_all | solution.py:94
  156.1 18.6 %all-reduce = s32[96]{0:T(128)S(1)} all-reduce(s32[96]{0:T(128)S(1)} %dynamic-update-slice), channel_id=1, replica_groups=mesh['pop'=8,'mp'=4] {'pop'}, use_global_device_ids=true, to_apply=%add | all-reduce | flops 96 | bytes 768
  177.4 20.4 %reshape.58 = bf16[4096,2,4,12]{3,2,1,0:T(4,128)(2,1)} reshape(bf16[8,2,24576]{2,1,0:T(2,128)(2,1)S(1)} %all-to-all-done) | data formatting | bytes 1572864
  197.8 12.0 %copy.72 = bf16[2,12,4,8,512]{4,2,1,3,0:T(4,128)(2,1)S(1)} copy(bf16[2,12,4,8,512]{1,2,0,4,3:T(4,128)(2,1)} %bitcast.74) | data formatting | bytes 1572864 | tf_op jit(solution)/shard_map/all_to_all | solution.py:94
  209.8 2.1 multiply_convert_fusion
  211.9 3.4 %bitcast_multiply_fusion = f32[2,1024,512]{2,1,0:T(8,128)} fusion(bf16[2,96,4,1024]{3,2,1,0:T(4,128)(2,1)S(1)} %multiply_convert_fusion, bf16[2,96,4,512]{3,2,1,0:T(4,128)(2,1)S(1)} %bitcast.76), kind=kOutput, calls=%fused_computation.8 | convolution fusion | flops 806354944 | bytes 6553600 | tf_op jit(solution)/shard_map/lmri,lmro->lio/dot_general | solution.py:99
  215.3 3.0 %add_convert_fusion.2 = bf16[16,12,4,1024]{3,2,1,0:T(4,128)(2,1)S(1)} fusion(f32[16,12,4,1024]{3,2,1,0:T(4,128)} %fusion.52, bf16[16,12,4,1024]{3,2,1,0:T(4,128)(2,1)S(1)} %copy-done.5, f32[1024]{0:T(1024)S(1)} %bitcast.113, f32[16,12,4]{2,1,0:T(8,128)S(1)} %copy.65), kind=kLoop, calls=%fused_computation.17 | loop fusion | flops 3932160 | bytes 6298624 | tf_op jit(solution)/shard_map/convert_element_type | solution.py:82
  218.4 1.9 fusion.26
  220.3 11.8 %psum.37 = f32[16,12,4,4]{0,3,2,1:T(4,128)S(1)} all-reduce(f32[16,12,4,4]{0,3,2,1:T(4,128)S(1)} %fusion.26), channel_id=1, replica_groups=mesh['pop'=8,'mp'=4] {'mp'}, use_global_device_ids=true, to_apply=%region_5.0 | all-reduce | flops 3072 | bytes 24576 | tf_op jit(solution)/shard_map/psum | solution.py:73
  232.1 3.1 %convolution_multiply_fusion = f32[12,1024,16,4]{1,2,3,0:T(8,128)} fusion(f32[16,12,4,4]{0,3,2,1:T(4,128)S(1)} %psum.37, bf16[2,12,4,4096]{3,2,1,0:T(4,128)(2,1)S(1)} %copy-done.7, s32[]{:T(128)S(6)} %add.456, s32[]{:T(128)S(6)} %select_n.3), kind=kOutput, calls=%fused_computation.20 | convolution fusion | flops 38535168 | bytes 3342344 | tf_op jit(solution)/shard_map/tmsr,mrd->tmsd/dot_general | solution.py:74
  235.2 4.1 %reshape.44 = f32[16,12,4,1024]{3,2,1,0:T(4,128)} reshape(bf16[768,1024]{1,0:T(8,128)(2,1)} %reduce-scatter.5.cloned.1.call-done) | data formatting | bytes 4718592 | tf_op jit(solution)/shard_map/reshape | solution.py:72
  239.3 5.3 %fusion.12 = f32[16,12,4,1024]{3,2,1,0:T(4,128)S(1)} fusion(f32[16,12,4,1024]{3,2,1,0:T(4,128)} %reshape.44, f32[12,1024,16,4]{1,2,3,0:T(8,128)} %convolution_multiply_fusion), kind=kLoop, calls=%fused_computation.10 | loop fusion | flops 786432 | bytes 9437184 | tf_op jit(solution)/shard_map/add | solution.py:77
  244.8 1.5 copy-done.3
  261.4 1.6 copy-done.4
  263.9 10.6 %psum.38 = f32[16,12,4]{0,2,1:T(4,128)S(1)} all-reduce(f32[16,12,4]{0,2,1:T(4,128)S(1)} %copy.85), channel_id=1, replica_groups=mesh['pop'=8,'mp'=4] {'mp'}, use_global_device_ids=true, to_apply=%region_7.0 | all-reduce | flops 768 | bytes 6144 | tf_op jit(solution)/shard_map/psum | solution.py:78
  274.7 3.1 %add_convert_fusion = bf16[16,12,4,1024]{3,2,1,0:T(4,128)(2,1)S(1)} fusion(f32[16,12,4,1024]{3,2,1,0:T(4,128)} %copy-done.4, bf16[16,12,4,1024]{3,2,1,0:T(4,128)(2,1)S(1)} %add_convert_fusion.2, f32[1024]{0:T(1024)S(1)} %bitcast.111, f32[16,12,4]{2,1,0:T(8,128)S(1)} %copy.70), kind=kLoop, calls=%fused_computation.14 | loop fusion | flops 3932160 | bytes 6298624 | tf_op jit(solution)/shard_map/convert_element_type | solution.py:82
  278.4 5.6 %fusion.14 = f32[1,16,12,4]{1,0,3,2:T(1,128)S(1)} fusion(f32[1024,1,1,1]{0,1,3,2:T(1,128)S(1)} %bitcast.114, bf16[16,12,4,1024]{3,2,1,0:T(4,128)(2,1)S(1)} %add_convert_fusion), kind=kOutput, calls=%fused_computation.23 | convolution fusion | flops 9437184 | bytes 1580032 | tf_op jit(solution)/shard_map/tmsd,d->tms/dot_general | solution.py:83
  284.0 10.5 %psum.39 = f32[16,12,4]{0,2,1:T(4,128)S(1)} all-reduce(f32[16,12,4]{0,2,1:T(4,128)S(1)} %bitcast.110), channel_id=1, replica_groups=mesh['pop'=8,'mp'=4] {'mp'}, use_global_device_ids=true, to_apply=%region_8.0 | all-reduce | flops 768 | bytes 6144 | tf_op jit(solution)/shard_map/psum | solution.py:86
  (80 shorter events, 24.6 us)
Async XLA Ops:
  8.0 1.1 copy-start
  8.0 8.7 %copy-start.10 = (f32[2,1024]{1,0:T(2,128)S(1)}, f32[2,1024]{1,0:T(2,128)}, u32[]{:S(2)}) copy-start(f32[2,1024]{1,0:T(2,128)} %param.15) | copy-start | bytes 24580
  8.0 8.8 %copy-start.11 = (f32[2,1024]{1,0:T(2,128)S(1)}, f32[2,1024]{1,0:T(2,128)}, u32[]{:S(2)}) copy-start(f32[2,1024]{1,0:T(2,128)} %param.16) | copy-start | bytes 24580
  8.0 8.8 %copy-start.9 = (s32[12,4,16]{2,1,0:T(4,128)S(1)}, s32[12,4,16]{2,1,0:T(4,128)}, u32[]{:S(2)}) copy-start(s32[12,4,16]{2,1,0:T(4,128)} %param.9) | copy-start | bytes 9220
  8.0 42.1 %reduce-scatter.3.cloned.1.call-start = ((), (), s32[]{:S(2)}) async-start(), calls=%async_computation.3 | async-start | bytes 2621440 | tf_op jit(solution)/shard_map/reduce_scatter | solution.py:23
  16.1 3.6 %copy-start.8 = (bf16[2,12,4,1024]{3,2,1,0:T(4,128)(2,1)S(1)}, bf16[2,12,4,1024]{3,2,1,0:T(4,128)(2,1)}, u32[]{:S(2)}) copy-start(bf16[2,12,4,1024]{3,2,1,0:T(4,128)(2,1)} %param.13) | copy-start | bytes 589828
  16.1 193.7 %all-gather.2.cloned.1.call-start = ((), (), s32[]{:S(2)}) async-start(), calls=%async_computation.5 | async-start | bytes 1769472 | tf_op jit(solution)/shard_map/all_gather | solution.py:96
  16.7 218.5 %reduce-scatter.5.cloned.1.call-start = ((), (), s32[]{:S(2)}) async-start(), calls=%async_computation.4 | async-start | bytes 7864320 | tf_op jit(solution)/shard_map/reduce_scatter | solution.py:23
  17.7 19.7 %copy-start.7 = (bf16[2,12,4,4096]{3,2,1,0:T(4,128)(2,1)S(1)}, bf16[2,12,4,4096]{3,2,1,0:T(4,128)(2,1)}, u32[]{:S(2)}) copy-start(bf16[2,12,4,4096]{3,2,1,0:T(4,128)(2,1)} %param.14) | copy-start | bytes 2359300
  50.2 1.7 copy-start.6
  64.3 1.8 copy-start.2
  131.2 23.5 %copy-start.14 = (u32[32]{0:T(128)S(1)}, u32[32]{0:T(128)}, u32[]{:S(2)}) copy-start(u32[32]{0:T(128)} %constant.44) | copy-start | bytes 388
  131.2 24.7 %copy-start.13 = (s32[12]{0:T(128)S(1)}, s32[12]{0:T(128)}, u32[]{:S(2)}) copy-start(s32[12]{0:T(128)} %param.10) | copy-start | bytes 148
  148.9 28.5 %all-to-all-start = ((bf16[8,2,24576]{2,1,0:T(2,128)(2,1)}), bf16[8,2,24576]{2,1,0:T(2,128)(2,1)S(1)}, u32[]{:S(2)}, u32[]{:S(2)}) async-start(bf16[8,2,24576]{2,1,0:T(2,128)(2,1)} %reshape.57), calls=%async_computation.2 | async-start | bytes 1572864 | tf_op jit(solution)/shard_map/all_to_all | solution.py:94
  211.9 3.5 %copy-start.5 = (bf16[16,12,4,1024]{3,2,1,0:T(4,128)(2,1)S(1)}, bf16[16,12,4,1024]{3,2,1,0:T(4,128)(2,1)}, u32[]{:S(2)}) copy-start(bf16[16,12,4,1024]{3,2,1,0:T(4,128)(2,1)} %reshape.39) | copy-start | bytes 4718596
  244.6 1.7 copy-start.3
  261.4 1.7 copy-start.4
  274.7 20.6 %copy-start.1 = (bf16[256,1024]{1,0:T(8,128)(2,1)S(1)}, bf16[256,1024]{1,0:T(8,128)(2,1)}, u32[]{:S(2)}) copy-start(bf16[256,1024]{1,0:T(8,128)(2,1)} %param.11) | copy-start | bytes 1572868
  274.7 3.7 %copy-start.12 = (f32[1024]{0:T(1024)S(1)}, f32[1024]{0:T(1024)}, u32[]{:S(2)}) copy-start(f32[1024]{0:T(1024)} %param.17) | copy-start | bytes 12292
Sparse Core Ops, SparseCore 0:
  16.2 33.8 reduce-scatter.2
  122.1 58.4 reduce-scatter.4
Sparse Core Ops, SparseCore 1:
  18.8 46.8 all-gather.1

commit v2 on v0

v2 whole, which is shorter than its diff:
```python
import functools

import jax
import jax.numpy as jnp
from jax import lax
from jax.experimental import pallas as pl
from jax.experimental.pallas import tpu as pltpu
from jax.sharding import PartitionSpec as P

noise_scale = 0.25
norm_eps = 1e-06
spread_eps = 1e-05
lanes = 128
f32, bf16 = jnp.float32, jnp.bfloat16


def policy_kernel(
    dims,
    onehot_ref,
    embed_ref,
    mix_ref,
    fin_ref,
    fout_ref,
    ranks_ref,
    decay_ref,
    gain_ref,
    reward_ref,
    final_ref,
    score_ref,
    gin_ref,
    gout_ref,
    granks_ref,
    weights,
    own_pair,
    got_pair,
    own_cross,
    got_cross,
    states,
    hidden,
    table,
    small,
    marks,
    weight_sem,
    pair_send,
    pair_recv,
    cross_send,
    cross_recv,
    small_send,
    small_recv,
    mark_send,
    mark_recv,
    pop_send,
    pop_recv,
    self_sem,
):
    pop, chunks, group, steps, member_rows, seqs, rank, width, full, coef = dims
    rows = group * steps
    vocab = embed_ref.shape[0]
    local = fin_ref.shape[1]
    columns = gout_ref.shape[2]
    mine = lax.axis_index("pop")
    me = lax.axis_index("mp")
    side, core = me // 2, me % 2
    mate = side * 2 + (1 - core)
    cross = (1 - side) * 2 + core
    diagonal = (1 - side) * 2 + (1 - core)
    others = (mate, cross, diagonal)
    blocks = (diagonal, cross, mate, me)

    def peer(q, j):
        return {"pop": q, "mp": j}

    def remote(src, dst, send, recv, q, j):
        return pltpu.make_async_remote_copy(
            src_ref=src,
            dst_ref=dst,
            send_sem=send,
            recv_sem=recv,
            device_id=peer(q, j),
            device_id_type=pl.DeviceIdType.MESH,
        )

    def weight_copy(layer, slot):
        start = pl.multiple_of(blocks[slot] * width, lanes)
        return pltpu.make_async_copy(
            mix_ref.at[layer, :, pl.ds(start, width)],
            weights.at[layer, slot],
            weight_sem.at[layer, slot],
        )

    for layer in range(2):
        for slot in range(4):
            weight_copy(layer, slot).start()

    barrier = pltpu.get_barrier_semaphore()
    for other in others:
        pl.semaphore_signal(
            barrier, inc=1, device_id=peer(mine, other), device_id_type=pl.DeviceIdType.MESH
        )

    def greet(hop, carry):
        pl.semaphore_signal(
            barrier,
            inc=1,
            device_id=peer(lax.rem(mine + hop, pop), me),
            device_id_type=pl.DeviceIdType.MESH,
        )
        return carry

    lax.fori_loop(1, pop, greet, 0)
    pl.semaphore_wait(barrier, 3 + pop - 1)

    def pop_copies(hop, source):
        target = lax.rem(mine + hop, pop)
        at = pl.multiple_of(source * local, local)
        cols = pl.multiple_of(target * columns, lanes)
        return (
            remote(
                fin_ref,
                gin_ref.at[:, pl.ds(at, local), :],
                pop_send.at[0, hop],
                pop_recv.at[0, hop],
                target,
                me,
            ),
            remote(
                fout_ref.at[:, :, pl.ds(cols, columns)],
                gout_ref.at[:, pl.ds(at, local), :],
                pop_send.at[1, hop],
                pop_recv.at[1, hop],
                target,
                me,
            ),
            remote(
                ranks_ref,
                granks_ref.at[source],
                pop_send.at[2, hop],
                pop_recv.at[2, hop],
                target,
                me,
            ),
        )

    def self_copies():
        at = pl.multiple_of(mine * local, local)
        cols = pl.multiple_of(mine * columns, lanes)
        return (
            pltpu.make_async_copy(fin_ref, gin_ref.at[:, pl.ds(at, local), :], self_sem.at[0]),
            pltpu.make_async_copy(
                fout_ref.at[:, :, pl.ds(cols, columns)],
                gout_ref.at[:, pl.ds(at, local), :],
                self_sem.at[1],
            ),
            pltpu.make_async_copy(ranks_ref, granks_ref.at[mine], self_sem.at[2]),
        )

    def send_pop(hop, carry):
        for copy in pop_copies(hop, mine):
            copy.start()
        return carry

    def small_copy(kind, g, r):
        return remote(
            small.at[kind, g, 0],
            small.at[kind, g, r + 1],
            small_send.at[kind, g, r],
            small_recv.at[kind, g, r],
            mine,
            others[r],
        )

    def small_start(kind, g, value):
        small[kind, g, 0] = value
        for r in range(3):
            small_copy(kind, g, r).start()

    def small_sum(kind, g):
        for r in range(3):
            small_copy(kind, g, r).wait_recv()
        return (small[kind, g, 0] + small[kind, g, 1]) + (small[kind, g, 2] + small[kind, g, 3])

    def pair_copy(k, slot):
        return remote(
            own_pair.at[k, slot],
            got_pair.at[k, slot],
            pair_send.at[k, slot],
            pair_recv.at[k, slot],
            mine,
            mate,
        )

    def cross_copy(k):
        return remote(
            own_cross.at[k], got_cross.at[k], cross_send.at[k], cross_recv.at[k], mine, cross
        )

    def mark_copy(g, r):
        return remote(
            marks.at[g, 0],
            marks.at[g, r + 1],
            mark_send.at[g, r],
            mark_recv.at[g, r],
            mine,
            others[r],
        )

    def exchange(k, read, count, layer, before):
        def product(slot):
            before(slot)
            return jnp.dot(read(), weights[layer, slot], preferred_element_type=f32).astype(bf16)

        own_pair[k, 0, :count] = product(0)
        pair_copy(k, 0).start()
        own_cross[k, :count] = product(1)
        pair_copy(k, 0).wait_recv()
        own_cross[k, :count] = (
            own_cross[k, :count].astype(f32) + got_pair[k, 0, :count].astype(f32)
        ).astype(bf16)
        cross_copy(k).start()
        own_pair[k, 1, :count] = product(2)
        pair_copy(k, 1).start()
        return product(3).astype(f32)

    def received(k, count):
        pair_copy(k, 1).wait_recv()
        cross_copy(k).wait_recv()
        return got_pair[k, 1, :count].astype(f32) + got_cross[k, :count].astype(f32)

    factor_rows = member_rows * rank
    mask = (lax.broadcasted_iota(jnp.int32, (factor_rows, rows), 0) // rank) == (
        (lax.broadcasted_iota(jnp.int32, (factor_rows, rows), 1) % group) // seqs
    )

    def factor_slice(ref, layer, g, start, size):
        at = pl.multiple_of(g * factor_rows, factor_rows)
        return ref[layer, pl.ds(at, factor_rows), pl.ds(start, size)]

    def low_start(layer, g, features):
        local_low = lax.dot_general(
            factor_slice(fin_ref, layer, g, 0, width),
            features,
            (((1,), (1,)), ((), ())),
            preferred_element_type=f32,
        )
        local_low = jnp.where(mask, local_low, 0.0)
        packed = local_low[:8]
        for at in range(8, factor_rows, 8):
            packed = packed + local_low[at : at + 8]
        small_start(layer, g, packed)

    def correction(layer, g):
        packed = small_sum(layer, g)
        low = jnp.concatenate([packed] * (factor_rows // 8), axis=0)
        low = jnp.where(mask, low, 0.0) * coef
        top = low.astype(bf16).astype(f32)
        blank = jnp.zeros((lanes - 2 * factor_rows, rows), f32)
        stacked = jnp.concatenate([top, low - top, blank], axis=0)
        factor = factor_slice(fout_ref, layer, g, pl.multiple_of(me * width, lanes), width)
        right = jnp.concatenate(
            [factor, factor, jnp.zeros((lanes - 2 * factor_rows, width), bf16)], axis=0
        )
        return jnp.dot(stacked.T.astype(bf16), right, preferred_element_type=f32)

    def recur(layer, g):
        decay = decay_ref[layer : layer + 1, :]
        kept = 1.0 - decay

        def advance(t, carried):
            at = pl.ds(pl.multiple_of(t * group, group), group)
            carried = decay * carried + kept * states[g, at, :]
            states[g, at, :] = carried
            return carried

        lax.fori_loop(0, steps, advance, jnp.zeros((group, width), f32), unroll=2)

        part = states[g, :, 0:lanes]
        total = part * part
        for t in range(1, width // lanes):
            part = states[g, :, t * lanes : (t + 1) * lanes]
            total = total + part * part
        total = total.T
        packed = total[:8]
        for at in range(8, lanes, 8):
            packed = packed + total[at : at + 8]
        small_start(2 + layer, g, packed)

    def normed(layer, g):
        squares = jnp.sum(small_sum(2 + layer, g), axis=0, keepdims=True)
        scale = lax.rsqrt(squares / full + norm_eps)
        scale = jnp.broadcast_to(scale, (lanes, rows)).T
        scale = jnp.concatenate([scale] * (width // lanes), axis=1)
        gain = gain_ref[layer : layer + 1, :]
        return (hidden[g].astype(f32) + states[g] * scale * gain).astype(bf16)

    first = exchange(
        0, lambda: embed_ref[...], vocab, 0, lambda slot: weight_copy(0, slot).wait()
    )
    lax.fori_loop(1, pop, send_pop, 0)
    for copy in self_copies():
        copy.start()

    def begin(g, carry):
        features = jnp.dot(onehot_ref[g], embed_ref[...], preferred_element_type=f32).astype(bf16)
        hidden[g] = features
        low_start(0, g, features)
        return carry

    lax.fori_loop(0, chunks, begin, 0)
    for slot in range(4):
        weight_copy(1, slot).wait()
    whole = first + received(0, vocab)
    top = whole.astype(bf16)
    table[0] = top
    table[1] = (whole - top.astype(f32)).astype(bf16)

    def layer_zero(g, carry):
        picks = onehot_ref[g]
        states[g] = (
            jnp.dot(picks, table[0], preferred_element_type=f32)
            + jnp.dot(picks, table[1], preferred_element_type=f32)
            + correction(0, g)
        )
        recur(0, g)
        return carry

    lax.fori_loop(0, chunks, layer_zero, 0)

    def between(g, carry):
        hidden[g] = normed(0, g)
        states[g] = exchange(1 + g, lambda: hidden[g], rows, 1, lambda slot: None)
        low_start(1, g, hidden[g])
        return carry

    lax.fori_loop(0, chunks, between, 0)

    def layer_one(g, carry):
        states[g] = states[g] + received(1 + g, rows) + correction(1, g)
        recur(1, g)
        return carry

    def finish(g, carry):
        last = normed(1, g)
        at = pl.ds(pl.multiple_of(g * group, group), group)
        final_ref[at, :] = last[rows - group :]
        total = last[:group].astype(f32)
        for t in range(1, steps):
            total = total + last[t * group : (t + 1) * group].astype(f32)
        total = total * reward_ref[...]
        packed = total[:, :lanes]
        for t in range(1, width // lanes):
            packed = packed + total[:, t * lanes : (t + 1) * lanes]
        marks[g, 0] = packed
        for r in range(3):
            mark_copy(g, r).start()
        return carry

    lax.fori_loop(0, chunks, lambda g, carry: finish(g, layer_one(g, carry)), 0)

    def collect(g, carry):
        for r in range(3):
            mark_copy(g, r).wait_recv()
        at = pl.ds(pl.multiple_of(g * group, group), group)
        score_ref[at, :] = (marks[g, 0] + marks[g, 1]) + (marks[g, 2] + marks[g, 3])
        for r in range(3):
            mark_copy(g, r).wait_send()
            for kind in range(4):
                small_copy(kind, g, r).wait_send()
        return carry

    lax.fori_loop(0, chunks, collect, 0)

    def drain(k, carry):
        pair_copy(k, 0).wait_send()
        pair_copy(k, 1).wait_send()
        cross_copy(k).wait_send()
        return carry

    lax.fori_loop(0, chunks + 1, drain, 0)

    def drain_pop(hop, carry):
        for copy in pop_copies(hop, lax.rem(mine + pop - hop, pop)):
            copy.wait_recv()
        for copy in pop_copies(hop, mine):
            copy.wait_send()
        return carry

    lax.fori_loop(1, pop, drain_pop, 0)
    for copy in self_copies():
        copy.wait()


def shards(
    token_ids,
    fitness_ranks,
    embedding,
    mix_weights,
    factors_in,
    factors_out,
    decay_rates,
    norm_gain,
    reward_dir,
):
    members, seqs, steps = token_ids.shape
    vocab, width = embedding.shape
    layers, _, full = mix_weights.shape
    rank = factors_in.shape[2]
    pop = lax.axis_size("pop")
    members_all = members * pop
    coef = noise_scale * (full * rank) ** (-0.5)
    columns = full // pop
    member_rows = 16 // seqs
    chunks = members // member_rows
    group = member_rows * seqs
    rows = group * steps
    local = members * rank
    ids = token_ids.reshape(chunks, member_rows, seqs, steps)
    ids = jnp.transpose(ids, (0, 3, 1, 2)).reshape(chunks, rows)
    onehot = (ids[:, :, None] == jnp.arange(vocab, dtype=jnp.int32)).astype(bf16)
    ranks = jnp.zeros((8, lanes), jnp.int32)
    ranks = lax.dynamic_update_slice(ranks, fitness_ranks[None, :], (0, 0))
    dims = (pop, chunks, group, steps, member_rows, seqs, rank, width, full, coef)
    vmem = pl.BlockSpec(memory_space=pltpu.VMEM)
    hbm = pl.BlockSpec(memory_space=pl.ANY)
    most = max(rows, vocab)
    phases = chunks + 1
    dma = pltpu.SemaphoreType.DMA
    final, marks, gin, gout, granks = pl.pallas_call(
        functools.partial(policy_kernel, dims),
        out_shape=(
            jax.ShapeDtypeStruct((members * seqs, width), bf16),
            jax.ShapeDtypeStruct((members * seqs, lanes), f32),
            jax.ShapeDtypeStruct((layers, pop * local, width), bf16),
            jax.ShapeDtypeStruct((layers, pop * local, columns), bf16),
            jax.ShapeDtypeStruct((pop, 8, lanes), jnp.int32),
        ),
        in_specs=[vmem, vmem, hbm, vmem, vmem, vmem, vmem, vmem, vmem],
        out_specs=(vmem, vmem, hbm, hbm, hbm),
        scratch_shapes=[
            pltpu.VMEM((layers, 4, width, width), bf16),
            pltpu.VMEM((phases, 2, most, width), bf16),
            pltpu.VMEM((phases, 2, most, width), bf16),
            pltpu.VMEM((phases, most, width), bf16),
            pltpu.VMEM((phases, most, width), bf16),
            pltpu.VMEM((chunks, rows, width), f32),
            pltpu.VMEM((chunks, rows, width), bf16),
            pltpu.VMEM((2, vocab, width), bf16),
            pltpu.VMEM((4, chunks, 4, 8, rows), f32),
            pltpu.VMEM((chunks, 4, group, lanes), f32),
            dma((layers, 4)),
            dma((phases, 2)),
            dma((phases, 2)),
            dma((phases,)),
            dma((phases,)),
            dma((4, chunks, 3)),
            dma((4, chunks, 3)),
            dma((chunks, 3)),
            dma((chunks, 3)),
            dma((3, pop)),
            dma((3, pop)),
            dma((3,)),
        ],
        compiler_params=pltpu.CompilerParams(
            collective_id=0, has_side_effects=True, vmem_limit_bytes=60 * 1024 * 1024
        ),
    )(
        onehot,
        embedding,
        mix_weights,
        factors_in.reshape(layers, local, width),
        factors_out.reshape(layers, local, full),
        ranks,
        decay_rates,
        norm_gain,
        reward_dir.reshape(1, width),
    )
    final_features = final.reshape(members, seqs, width)
    scores = jnp.sum(marks, axis=1).reshape(members, seqs) * (full ** (-0.5) / steps)
    ranks_every = granks[:, 0, :members].reshape(-1)
    shares_all = ranks_every.astype(f32) / members_all
    rank_mean = jnp.mean(shares_all)
    rank_spread = jnp.mean((shares_all - rank_mean) * (shares_all - rank_mean)) + spread_eps
    shaped_all = (shares_all - rank_mean) * lax.rsqrt(rank_spread)
    shaped_rows = jnp.repeat(shaped_all, rank)
    weighted = (gin.astype(f32) * shaped_rows[None, :, None]).astype(bf16)
    weight_delta = jnp.einsum("lki,lko->lio", weighted, gout, preferred_element_type=f32)
    weight_step = weight_delta * (members_all * rank) ** (-0.5)
    return (final_features, scores, weight_step)


def solution(mesh):
    return jax.shard_map(
        shards,
        mesh=mesh,
        in_specs=(
            P("pop", None, None),
            P("pop"),
            P(None, "mp"),
            P(None, "mp", None),
            P(None, "pop", None, "mp"),
            P(None, "pop", None, None),
            P(None, "mp"),
            P(None, "mp"),
            P("mp"),
        ),
        out_specs=(P("pop", None, "mp"), P("pop", None), P(None, "mp", "pop")),
        check_vma=False,
    )
```

time: 491 us -> 102 us (0.21)
  local copies, waits for them, and re-layouts: 278 us -> 8.77 us
  Pallas kernels: 0 us -> 80.2 us
  blocking collectives: 75.3 us -> 0 us
  waiting for transfers between devices: 44.5 us -> 0 us
  matrix products: 46.3 us -> 5 us
  between operations: 17.7 us -> 2 us
  other arithmetic: 17 us -> 5.3 us
  starting transfers between devices: 5.72 us -> 0 us
    dynamic_update_slice x64 -> x1, local copies, waits for them, and re-layouts: 161 us -> 1.25 us  [shards(): ranks = lax.dynamic_update_slice(ranks, fitness_ranks[None, :], (0, 0))]
    pallas_call x0 -> x1, Pallas kernels: none -> 80.2 us  [shards(): pl.pallas_call(functools.partial(policy_kernel, dims), out_shape=(jax.Sha...]
    psum x5 -> x0, blocking collectives: 56.7 us -> none  [the longest x2 25.2 us: shards(): low_rank = lax.psum(project_rank(hidden, factors_in[layer_idx]), 'mp')]
    dynamic_slice x32 -> x0, local copies, waits for them, and re-layouts: 50.3 us -> none  [recurrence(): _, states = lax.scan(advance, initial, time_major)]
    unnamed x28 -> x1, local copies, waits for them, and re-layouts: 49.7 us -> 0.68 us
    reduce_scatter x2 -> x0, waiting for transfers between devices: 44 us -> none  [mixed_inputs(): lax.psum_scatter(partial_value.astype(jnp.bfloat16), 'mp', scatter_dimens...]
    dot_general x9 -> x1, matrix products: 46.3 us -> 5 us  [shards(): jnp.einsum('lki,lko->lio', weighted, gout, preferred_element_type=f32)]
    unnamed x1 -> x0, blocking collectives: 18.6 us -> none
  transfers between devices with their start and end apart: 4 -> 0, of which waited for: 1 -> 0; matrix products, arithmetic and copies ran while one was open for 41% -> 0% of each run, Pallas kernels for 0% -> 0%
where the time goes in v2:
time: 102 us; the launch traced here: 101 us
  Pallas kernels  80.2 us (79%)
  local copies, waits for them, and re-layouts  8.77 us (9%)
  other arithmetic  5.3 us (5%)
  matrix products  5 us (5%)
  between operations  2 us (2%)
    pallas_call x1, Pallas kernels, shards(): pl.pallas_call(functools.partial(policy_kernel, dims), out_shape=(jax.Sha...  80.2 us
    dot_general x1, matrix products, shards(): jnp.einsum('lki,lko->lio', weighted, gout, preferred_element_type=f32)  5 us
    reshape x1, local copies, waits for them, and re-layouts, shards(): factors_out.reshape(layers, local, full)  2.25 us

profile of v2, /device:TPU:0, one launch (start us, length us, event | category | flops | bytes accessed | tf_op | source)
XLA Modules:
  0.0 101.3 jit_solution(7281215413892971518)
XLA Ops:
  0.6 1.3 %dynamic_update_slice.3.ranks_ref = s32[8,128]{1,0:T(8,128)} pad(s32[1,12]{1,0:T(1,128)} %bitcast.8, s32[]{:T(128)} %constant.6.clone.1), padding=0_7x0_116 | pad | bytes 4148 | tf_op jit(solution)/shard_map/dynamic_update_slice | solution.py:420
  1.9 0.9 copy.15
  2.8 0.1 eq.15
  2.9 1.7 %reshape.34.fin_ref = bf16[2,48,1024]{2,1,0:T(8,128)(2,1)} reshape(bf16[2,12,4,1024]{3,2,1,0:T(4,128)(2,1)} %param.13) | data formatting | bytes 393216 | tf_op jit(solution)/shard_map/reshape | solution.py:469
  4.6 0.9 fusion.1.onehot_ref
  5.5 2.3 %reshape.35.fout_ref = bf16[2,48,4096]{2,1,0:T(8,128)(2,1)} reshape(bf16[2,12,4,4096]{3,2,1,0:T(4,128)(2,1)} %param.14) | data formatting | bytes 1572864 | tf_op jit(solution)/shard_map/reshape | solution.py:470
  7.7 80.2 %shard_map.112 = (bf16[48,1024]{1,0:T(8,128)(2,1)}, f32[48,128]{1,0:T(8,128)}, bf16[2,384,1024]{2,1,0:T(8,128)(2,1)}, bf16[2,384,512]{2,1,0:T(8,128)(2,1)}, s32[8,8,128]{2,1,0:T(8,128)}) custom-call(bf16[3,256,256]{2,1,0:T(8,128)(2,1)} %fusion.1.onehot_ref, bf16[256,1024]{1,0:T(8,128)(2,1)} %embed_ref.1, bf16[2,1024,4096]{2,1,0:T(8,128)(2,1)} %mix_ref.1, ...), custom_call_target="tpu_custom_call" | custom-call | tf_op jit(solution)/shard_map/pallas_call | solution.py:427
  87.9 1.4 %fusion.2 = f32[]{:T(128)} fusion(s32[8,8,128]{2,1,0:T(8,128)} %get-tuple-element.11), kind=kLoop, calls=%fused_computation.9 | loop fusion | flops 287 | bytes 388 | tf_op jit(solution)/shard_map/reduce_sum | solution.py:480
  90.0 1.4 %multiply_reduce_fusion.1 = f32[]{:T(128)} fusion(f32[]{:T(128)S(6)} %div.14, s32[8,8,128]{2,1,0:T(8,128)} %get-tuple-element.11), kind=kLoop, calls=%fused_computation.6 | loop fusion | flops 479 | bytes 392 | tf_op jit(solution)/shard_map/reduce_sum | solution.py:481
  92.0 1.6 %reshape.37 = bf16[12,4,1024]{2,1,0:T(4,128)(2,1)} reshape(bf16[48,1024]{1,0:T(8,128)(2,1)} %get-tuple-element.8) | data formatting | bytes 196608 | tf_op jit(solution)/shard_map/reshape | solution.py:476
  93.6 0.8 reduce_sum.27
  94.5 0.8 multiply_reduce_fusion
  95.3 0.1 mul.44
  95.3 0.1 mul.40
  95.4 0.7 copy.17
  96.1 0.1 broadcast_in_dim.9
  96.2 0.1 mul.45
  96.3 5.0 %convolution_multiply_fusion = f32[2,1024,512]{2,1,0:T(8,128)} fusion(bf16[2,384,512]{2,1,0:T(8,128)(2,1)} %get-tuple-element.12, bf16[2,384,1024]{2,1,0:T(8,128)(2,1)} %get-tuple-element.10, f32[384]{0:T(512)S(1)} %mul.45), kind=kOutput, calls=%fused_computation.1 | convolution fusion | flops 808714240 | bytes 6555136 | tf_op jit(solution)/shard_map/lki,lko->lio/dot_general | solution.py:485
  (1 shorter events, 0.0 us)

commit v3 on v2

v3 whole, which is shorter than its diff:
```python
import functools

import jax
import jax.numpy as jnp
from jax import lax
from jax.experimental import pallas as pl
from jax.experimental.pallas import tpu as pltpu
from jax.sharding import PartitionSpec as P

noise_scale = 0.25
norm_eps = 1e-06
spread_eps = 1e-05
lanes = 128
f32, bf16 = jnp.float32, jnp.bfloat16


def policy_kernel(
    dims,
    onehot_ref,
    embed_ref,
    mix_ref,
    fin_raw,
    fout_raw,
    ranks_smem,
    decay_ref,
    gain_ref,
    reward_ref,
    final_ref,
    score_ref,
    gin_ref,
    gout_ref,
    weights,
    own_pair,
    got_pair,
    own_cross,
    got_cross,
    states,
    hidden,
    fin_ref,
    fout_ref,
    scaled,
    ranks,
    granks_ref,
    lows,
    squares,
    small,
    marks,
    weight_sem,
    pair_send,
    pair_recv,
    cross_send,
    cross_recv,
    small_send,
    small_recv,
    mark_send,
    mark_recv,
    pop_send,
    pop_recv,
    self_sem,
):
    pop, chunks, group, steps, member_rows, seqs, rank, width, full, coef = dims
    parts = pair_send.shape[2]
    piece = width // parts
    halves = [slice(p * piece, (p + 1) * piece) for p in range(parts)]
    rows = group * steps
    vocab = embed_ref.shape[0]
    local = fin_ref.shape[1]
    columns = gout_ref.shape[2]
    mine = lax.axis_index("pop")
    me = lax.axis_index("mp")
    side, core = me // 2, me % 2
    mate = side * 2 + (1 - core)
    cross = (1 - side) * 2 + core
    diagonal = (1 - side) * 2 + (1 - core)
    others = (mate, cross, diagonal)
    blocks = (diagonal, cross, mate, me)

    def peer(q, j):
        return {"pop": q, "mp": j}

    def remote(src, dst, send, recv, q, j):
        return pltpu.make_async_remote_copy(
            src_ref=src,
            dst_ref=dst,
            send_sem=send,
            recv_sem=recv,
            device_id=peer(q, j),
            device_id_type=pl.DeviceIdType.MESH,
        )

    def weight_copy(layer, slot):
        start = pl.multiple_of(blocks[slot] * width, lanes)
        return pltpu.make_async_copy(
            mix_ref.at[layer, :, pl.ds(start, width)],
            weights.at[layer, slot],
            weight_sem.at[layer, slot],
        )

    for layer in range(2):
        for slot in range(4):
            weight_copy(layer, slot).start()

    barrier = pltpu.get_barrier_semaphore()
    for other in others:
        pl.semaphore_signal(
            barrier, inc=1, device_id=peer(mine, other), device_id_type=pl.DeviceIdType.MESH
        )

    def greet(hop, carry):
        pl.semaphore_signal(
            barrier,
            inc=1,
            device_id=peer(lax.rem(mine + hop, pop), me),
            device_id_type=pl.DeviceIdType.MESH,
        )
        return carry

    lax.fori_loop(1, pop, greet, 0)
    pl.semaphore_wait(barrier, 3 + pop - 1)

    members = ranks_smem.shape[0]
    members_all = members * pop

    def rank_copy(hop, source):
        return remote(
            ranks,
            granks_ref.at[source],
            pop_send.at[2, hop],
            pop_recv.at[2, hop],
            lax.rem(mine + hop, pop),
            me,
        )

    def out_copy(hop, source):
        target = lax.rem(mine + hop, pop)
        at = pl.multiple_of(source * local, local)
        cols = pl.multiple_of(target * columns, lanes)
        return remote(
            fout_ref.at[:, :, pl.ds(cols, columns)],
            gout_ref.at[:, pl.ds(at, local), :],
            pop_send.at[1, hop],
            pop_recv.at[1, hop],
            target,
            me,
        )

    def in_copy(hop, source):
        at = pl.multiple_of(source * local, local)
        return remote(
            scaled,
            gin_ref.at[:, pl.ds(at, local), :],
            pop_send.at[0, hop],
            pop_recv.at[0, hop],
            lax.rem(mine + hop, pop),
            me,
        )

    def self_copies():
        at = pl.multiple_of(mine * local, local)
        cols = pl.multiple_of(mine * columns, lanes)
        return (
            pltpu.make_async_copy(scaled, gin_ref.at[:, pl.ds(at, local), :], self_sem.at[0]),
            pltpu.make_async_copy(
                fout_ref.at[:, :, pl.ds(cols, columns)],
                gout_ref.at[:, pl.ds(at, local), :],
                self_sem.at[1],
            ),
        )

    def send_with(make):
        def send(hop, carry):
            make(hop, mine).start()
            return carry

        lax.fori_loop(1, pop, send, 0)

    def rank_block(shape, axis, repeats):
        index = lax.broadcasted_iota(jnp.int32, shape, axis)
        block = jnp.zeros(shape, jnp.int32)
        for m in range(members):
            block = jnp.where(index // repeats == m, ranks_smem[m], block)
        return block

    ranks[...] = rank_block((8, lanes), 1, 1)
    send_with(rank_copy)
    granks_ref[mine] = ranks[...]

    def unpack(g, carry):
        at = pl.ds(pl.multiple_of(g * member_rows * rank, member_rows * rank), member_rows * rank)
        for layer in range(2):
            for raw, ref in ((fin_raw, fin_ref), (fout_raw, fout_ref)):
                ref[layer, at, :] = jnp.concatenate(
                    [raw[layer, g * member_rows + m].astype(f32) for m in range(member_rows)],
                    axis=0,
                ).astype(bf16)
        return carry

    def shape_ranks():
        def arrived(hop, carry):
            rank_copy(hop, lax.rem(mine + pop - hop, pop)).wait_recv()
            return carry

        lax.fori_loop(1, pop, arrived, 0)
        full_block = (pop, 8, lanes)
        kept = (lax.broadcasted_iota(jnp.int32, full_block, 1) == 0) & (
            lax.broadcasted_iota(jnp.int32, full_block, 2) < members
        )
        shares = jnp.where(kept, granks_ref[...].astype(f32) / members_all, 0.0)

        def mean_of(value):
            value = jnp.sum(value, axis=0)
            value = jnp.sum(value, axis=0, keepdims=True)
            return jnp.sum(value, axis=1, keepdims=True) / members_all

        rank_mean = mean_of(shares)
        apart = jnp.where(kept, shares - rank_mean[None], 0.0)
        spread = mean_of(apart * apart) + spread_eps
        own = rank_block((local, lanes), 0, rank).astype(f32) / members_all
        shaped = (own - rank_mean) * lax.rsqrt(spread)
        shaped = jnp.concatenate([shaped] * (width // lanes), axis=1)
        for layer in range(2):
            scaled[layer] = (fin_ref[layer].astype(f32) * shaped).astype(bf16)

    def small_copy(kind, g, r):
        return remote(
            small.at[kind, g, 0],
            small.at[kind, g, r + 1],
            small_send.at[kind, g, r],
            small_recv.at[kind, g, r],
            mine,
            others[r],
        )

    def small_start(kind, g, value):
        small[kind, g, 0] = value
        for r in range(3):
            small_copy(kind, g, r).start()

    def small_sum(kind, g):
        for r in range(3):
            small_copy(kind, g, r).wait_recv()
        return (small[kind, g, 0] + small[kind, g, 1]) + (small[kind, g, 2] + small[kind, g, 3])

    def pair_copy(k, slot, p):
        return remote(
            own_pair.at[k, slot, p],
            got_pair.at[k, slot, p],
            pair_send.at[k, slot, p],
            pair_recv.at[k, slot, p],
            mine,
            mate,
        )

    def cross_copy(k, p):
        return remote(
            own_cross.at[k, p],
            got_cross.at[k, p],
            cross_send.at[k, p],
            cross_recv.at[k, p],
            mine,
            cross,
        )

    def mark_copy(g, r):
        return remote(
            marks.at[g, 0],
            marks.at[g, r + 1],
            mark_send.at[g, r],
            mark_recv.at[g, r],
            mine,
            others[r],
        )

    def exchange(k, read, count, layer, before, put):
        def product(slot, p):
            return jnp.dot(
                read(), weights[layer, slot, :, halves[p]], preferred_element_type=f32
            ).astype(bf16)

        before(0)
        for p in range(parts):
            own_pair[k, 0, p, :count] = product(0, p)
            pair_copy(k, 0, p).start()
        before(1)
        for p in range(parts):
            value = product(1, p).astype(f32)
            pair_copy(k, 0, p).wait_recv()
            own_cross[k, p, :count] = (value + got_pair[k, 0, p, :count].astype(f32)).astype(bf16)
            cross_copy(k, p).start()
        before(2)
        for p in range(parts):
            own_pair[k, 1, p, :count] = product(2, p)
            pair_copy(k, 1, p).start()
        before(3)
        for p in range(parts):
            put(halves[p], product(3, p).astype(f32))

    def received(k, count, p):
        pair_copy(k, 1, p).wait_recv()
        cross_copy(k, p).wait_recv()
        return got_pair[k, 1, p, :count].astype(f32) + got_cross[k, p, :count].astype(f32)

    factor_rows = member_rows * rank
    mask = (lax.broadcasted_iota(jnp.int32, (factor_rows, rows), 0) // rank) == (
        (lax.broadcasted_iota(jnp.int32, (factor_rows, rows), 1) % group) // seqs
    )

    def factor_slice(ref, layer, g, start, size):
        at = pl.multiple_of(g * factor_rows, factor_rows)
        return ref[layer, pl.ds(at, factor_rows), pl.ds(start, size)]

    def low_start(layer, g, features):
        local_low = lax.dot_general(
            factor_slice(fin_ref, layer, g, 0, width),
            features,
            (((1,), (1,)), ((), ())),
            preferred_element_type=f32,
        )
        local_low = jnp.where(mask, local_low, 0.0)
        packed = local_low[:8]
        for at in range(8, factor_rows, 8):
            packed = packed + local_low[at : at + 8]
        small_start(layer, g, packed)

    def low_ready(layer, g):
        packed = small_sum(layer, g)
        low = jnp.concatenate([packed] * (factor_rows // 8), axis=0)
        low = jnp.where(mask, low, 0.0) * coef
        top = low.astype(bf16).astype(f32)
        blank = jnp.zeros((lanes - 2 * factor_rows, rows), f32)
        lows[g] = jnp.concatenate([top, low - top, blank], axis=0).T.astype(bf16)

    def correction(layer, g, p):
        start = pl.multiple_of(me * width + p * piece, lanes)
        factor = factor_slice(fout_ref, layer, g, start, piece)
        right = jnp.concatenate(
            [factor, factor, jnp.zeros((lanes - 2 * factor_rows, piece), bf16)], axis=0
        )
        return jnp.dot(lows[g], right, preferred_element_type=f32)

    def recur(layer, g, p, inputs):
        decay = decay_ref[layer : layer + 1, halves[p]]
        kept = 1.0 - decay
        carried = jnp.zeros((group, piece), f32)
        for t in range(steps):
            at = slice(t * group, (t + 1) * group)
            carried = decay * carried + kept * inputs[at]
            states[g, at, halves[p]] = carried
            powers = carried * carried
            total = powers[:, :lanes]
            for c in range(lanes, piece, lanes):
                total = total + powers[:, c : c + lanes]
            if p:
                total = total + squares[g, at, :]
            squares[g, at, :] = total

    def squares_start(layer, g):
        total = squares[g].T
        packed = total[:8]
        for at in range(8, lanes, 8):
            packed = packed + total[at : at + 8]
        small_start(2 + layer, g, packed)

    def normed(layer, g):
        squares = jnp.sum(small_sum(2 + layer, g), axis=0, keepdims=True)
        scale = lax.rsqrt(squares / full + norm_eps)
        scale = jnp.broadcast_to(scale, (lanes, rows)).T
        scale = jnp.concatenate([scale] * (width // lanes), axis=1)
        gain = gain_ref[layer : layer + 1, :]
        return (hidden[g].astype(f32) + states[g, :rows] * scale * gain).astype(bf16)

    def put_first(cols, value):
        states[0, :vocab, cols] = value

    exchange(
        0,
        lambda: embed_ref[...],
        vocab,
        0,
        lambda slot: weight_copy(0, slot).wait(),
        put_first,
    )
    lax.fori_loop(0, chunks, unpack, 0)
    send_with(out_copy)

    def begin(g, carry):
        features = jnp.dot(onehot_ref[g], embed_ref[...], preferred_element_type=f32).astype(bf16)
        hidden[g] = features
        low_start(0, g, features)
        return carry

    lax.fori_loop(0, chunks, begin, 0)
    shape_ranks()
    send_with(in_copy)
    for copy in self_copies():
        copy.start()
    for slot in range(4):
        weight_copy(1, slot).wait()

    def low_zero(g, carry):
        low_ready(0, g)
        return carry

    lax.fori_loop(0, chunks, low_zero, 0)
    for p in range(parts):
        whole = states[0, :vocab, halves[p]] + received(0, vocab, p)
        top = whole.astype(bf16)
        rest = (whole - top.astype(f32)).astype(bf16)

        def layer_zero(g, carry, p=p, top=top, rest=rest):
            picks = onehot_ref[g]
            inputs = (
                jnp.dot(picks, top, preferred_element_type=f32)
                + jnp.dot(picks, rest, preferred_element_type=f32)
                + correction(0, g, p)
            )
            recur(0, g, p, inputs)
            if p == parts - 1:
                squares_start(0, g)
            return carry

        for g in range(chunks):
            layer_zero(g, 0)

    def between(g, carry):
        hidden[g] = normed(0, g)

        def put(cols, value):
            states[g, :rows, cols] = value

        exchange(1 + g, lambda: hidden[g], rows, 1, lambda slot: None, put)
        low_start(1, g, hidden[g])
        return carry

    lax.fori_loop(0, chunks, between, 0)

    def layer_one(g, carry):
        low_ready(1, g)
        for p in range(parts):
            inputs = states[g, :rows, halves[p]] + received(1 + g, rows, p) + correction(1, g, p)
            recur(1, g, p, inputs)
        squares_start(1, g)
        return carry

    def finish(g, carry):
        last = normed(1, g)
        at = pl.ds(pl.multiple_of(g * group, group), group)
        final_ref[at, :] = last[rows - group :]
        total = last[:group].astype(f32)
        for t in range(1, steps):
            total = total + last[t * group : (t + 1) * group].astype(f32)
        total = total * reward_ref[...]
        packed = total[:, :lanes]
        for t in range(1, width // lanes):
            packed = packed + total[:, t * lanes : (t + 1) * lanes]
        marks[g, 0] = packed
        for r in range(3):
            mark_copy(g, r).start()
        return carry

    lax.fori_loop(0, chunks, lambda g, carry: finish(g, layer_one(g, carry)), 0)

    def collect(g, carry):
        for r in range(3):
            mark_copy(g, r).wait_recv()
        at = pl.ds(pl.multiple_of(g * group, group), group)
        score_ref[at, :] = (marks[g, 0] + marks[g, 1]) + (marks[g, 2] + marks[g, 3])
        for r in range(3):
            mark_copy(g, r).wait_send()
            for kind in range(4):
                small_copy(kind, g, r).wait_send()
        return carry

    lax.fori_loop(0, chunks, collect, 0)

    def drain(k, carry):
        for p in range(parts):
            pair_copy(k, 0, p).wait_send()
            pair_copy(k, 1, p).wait_send()
            cross_copy(k, p).wait_send()
        return carry

    lax.fori_loop(0, chunks + 1, drain, 0)

    def drain_pop(hop, carry):
        source = lax.rem(mine + pop - hop, pop)
        in_copy(hop, source).wait_recv()
        out_copy(hop, source).wait_recv()
        for make in (rank_copy, in_copy, out_copy):
            make(hop, mine).wait_send()
        return carry

    lax.fori_loop(1, pop, drain_pop, 0)
    for copy in self_copies():
        copy.wait()


def shards(
    token_ids,
    fitness_ranks,
    embedding,
    mix_weights,
    factors_in,
    factors_out,
    decay_rates,
    norm_gain,
    reward_dir,
):
    members, seqs, steps = token_ids.shape
    vocab, width = embedding.shape
    layers, _, full = mix_weights.shape
    rank = factors_in.shape[2]
    pop = lax.axis_size("pop")
    members_all = members * pop
    coef = noise_scale * (full * rank) ** (-0.5)
    columns = full // pop
    member_rows = 16 // seqs
    chunks = members // member_rows
    group = member_rows * seqs
    rows = group * steps
    local = members * rank
    ids = token_ids.reshape(chunks, member_rows, seqs, steps)
    ids = jnp.transpose(ids, (0, 3, 1, 2)).reshape(chunks, rows)
    onehot = (ids[:, :, None] == jnp.arange(vocab, dtype=jnp.int32)).astype(bf16)
    dims = (pop, chunks, group, steps, member_rows, seqs, rank, width, full, coef)
    vmem = pl.BlockSpec(memory_space=pltpu.VMEM)
    smem = pl.BlockSpec(memory_space=pltpu.SMEM)
    hbm = pl.BlockSpec(memory_space=pl.ANY)
    most = max(rows, vocab)
    phases = chunks + 1
    parts = 4
    dma = pltpu.SemaphoreType.DMA
    final, marks, gin, gout = pl.pallas_call(
        functools.partial(policy_kernel, dims),
        out_shape=(
            jax.ShapeDtypeStruct((members * seqs, width), bf16),
            jax.ShapeDtypeStruct((members * seqs, lanes), f32),
            jax.ShapeDtypeStruct((layers, pop * local, width), bf16),
            jax.ShapeDtypeStruct((layers, pop * local, columns), bf16),
        ),
        in_specs=[vmem, vmem, hbm, vmem, vmem, smem, vmem, vmem, vmem],
        out_specs=(vmem, vmem, hbm, hbm),
        scratch_shapes=[
            pltpu.VMEM((layers, 4, width, width), bf16),
            pltpu.VMEM((phases, 2, parts, most, width // parts), bf16),
            pltpu.VMEM((phases, 2, parts, most, width // parts), bf16),
            pltpu.VMEM((phases, parts, most, width // parts), bf16),
            pltpu.VMEM((phases, parts, most, width // parts), bf16),
            pltpu.VMEM((chunks, most, width), f32),
            pltpu.VMEM((chunks, rows, width), bf16),
            pltpu.VMEM((layers, local, width), bf16),
            pltpu.VMEM((layers, local, full), bf16),
            pltpu.VMEM((layers, local, width), bf16),
            pltpu.VMEM((8, lanes), jnp.int32),
            pltpu.VMEM((pop, 8, lanes), jnp.int32),
            pltpu.VMEM((chunks, rows, lanes), bf16),
            pltpu.VMEM((chunks, rows, lanes), f32),
            pltpu.VMEM((4, chunks, 4, 8, rows), f32),
            pltpu.VMEM((chunks, 4, group, lanes), f32),
            dma((layers, 4)),
            dma((phases, 2, parts)),
            dma((phases, 2, parts)),
            dma((phases, parts)),
            dma((phases, parts)),
            dma((4, chunks, 3)),
            dma((4, chunks, 3)),
            dma((chunks, 3)),
            dma((chunks, 3)),
            dma((3, pop)),
            dma((3, pop)),
            dma((2,)),
        ],
        compiler_params=pltpu.CompilerParams(
            collective_id=0, has_side_effects=True, vmem_limit_bytes=60 * 1024 * 1024
        ),
    )(
        onehot,
        embedding,
        mix_weights,
        factors_in,
        factors_out,
        fitness_ranks,
        decay_rates,
        norm_gain,
        reward_dir.reshape(1, width),
    )
    final_features = final.reshape(members, seqs, width)
    scores = jnp.sum(marks, axis=1).reshape(members, seqs) * (full ** (-0.5) / steps)
    weight_delta = jnp.einsum("lki,lko->lio", gin, gout, preferred_element_type=f32)
    weight_step = weight_delta * (members_all * rank) ** (-0.5)
    return (final_features, scores, weight_step)


def solution(mesh):
    return jax.shard_map(
        shards,
        mesh=mesh,
        in_specs=(
            P("pop", None, None),
            P("pop"),
            P(None, "mp"),
            P(None, "mp", None),
            P(None, "pop", None, "mp"),
            P(None, "pop", None, None),
            P(None, "mp"),
            P(None, "mp"),
            P("mp"),
        ),
        out_specs=(P("pop", None, "mp"), P("pop", None), P(None, "mp", "pop")),
        check_vma=False,
    )
```

time: 102 us -> 93.2 us (0.914)
  local copies, waits for them, and re-layouts: 8.77 us -> 3.36 us
  other arithmetic: 5.3 us -> 1.77 us
  Pallas kernels: 80.2 us -> 82.1 us
  between operations: 2 us -> 0.65 us
    reshape x2 -> x0, local copies, waits for them, and re-layouts: 3.9 us -> none  [the longest x1 2.25 us: shards(): factors_out.reshape(layers, local, full)]
    reduce_sum x2 -> x0, other arithmetic: 2.75 us -> none  [the longest x1 1.38 us: shards(): jnp.mean((shares_all - rank_mean) * (shares_all - rank_mean)) + spread_eps]
    pallas_call x1, Pallas kernels: 80.2 us -> 82.1 us  [shards(): pl.pallas_call(functools.partial(policy_kernel, dims), out_shape=(jax.Sha...]
    dynamic_update_slice x1 -> x0, local copies, waits for them, and re-layouts: 1.25 us -> none  [shards(): ranks = lax.dynamic_update_slice(ranks, fitness_ranks[None, :], (0, 0))]
where the time goes in v3:
time: 93.2 us; the launch traced here: 92.8 us
  Pallas kernels  82.1 us (88%)
  matrix products  4.91 us (5%)
  local copies, waits for them, and re-layouts  3.36 us (4%)
  other arithmetic  1.77 us (2%)
    pallas_call x1, Pallas kernels, shards(): pl.pallas_call(functools.partial(policy_kernel, dims), out_shape=(jax.Sha...  82.1 us
    dot_general x1, matrix products, shards(): jnp.einsum('lki,lko->lio', gin, gout, preferred_element_type=f32)  4.91 us

profile of v3, /device:TPU:0, one launch (start us, length us, event | category | flops | bytes accessed | tf_op | source)
XLA Modules:
  0.0 92.8 jit_solution(14938041401801183827)
XLA Ops:
  0.6 0.9 copy.15
  1.5 0.1 eq.15
  1.7 0.9 fusion.onehot_ref
  2.6 82.1 %shard_map.112 = (bf16[48,1024]{1,0:T(8,128)(2,1)}, f32[48,128]{1,0:T(8,128)}, bf16[2,384,1024]{2,1,0:T(8,128)(2,1)}, bf16[2,384,512]{2,1,0:T(8,128)(2,1)}) custom-call(bf16[3,256,256]{2,1,0:T(8,128)(2,1)} %fusion.onehot_ref, bf16[256,1024]{1,0:T(8,128)(2,1)} %embed_ref.1, bf16[2,1024,4096]{2,1,0:T(8,128)(2,1)} %mix_ref.1, bf16[2,12,4,1024]{3,2,1,0:T(4,128)(2,1)} %fin_raw.1, ...), custom_call_target="tpu_custom_call" | custom-call | tf_op jit(solution)/shard_map/pallas_call | solution.py:533
  84.7 1.6 %reshape.21 = bf16[12,4,1024]{2,1,0:T(4,128)(2,1)} reshape(bf16[48,1024]{1,0:T(8,128)(2,1)} %get-tuple-element.7) | data formatting | bytes 196608 | tf_op jit(solution)/shard_map/reshape | solution.py:587
  86.3 0.8 reduce_sum.9
  87.2 0.1 mul.17
  87.2 0.7 copy.17
  87.9 4.9 %convolution_multiply_fusion = f32[2,1024,512]{2,1,0:T(8,128)} fusion(bf16[2,384,1024]{2,1,0:T(8,128)(2,1)} %get-tuple-element.9, bf16[2,384,512]{2,1,0:T(8,128)(2,1)} %get-tuple-element.10), kind=kOutput, calls=%fused_computation | convolution fusion | flops 806354944 | bytes 6553600 | tf_op jit(solution)/shard_map/lki,lko->lio/dot_general | solution.py:589
  (1 shorter events, 0.0 us)

commit v4 on v3

--- a/solution.py
+++ b/solution.py
@@ -16,11 +16,11 @@
 
 def policy_kernel(
     dims,
-    onehot_ref,
+    ids_ref,
     embed_ref,
     mix_ref,
     fin_raw,
-    fout_raw,
+    fout_hbm,
     ranks_smem,
     decay_ref,
     gain_ref,
@@ -36,6 +36,8 @@
     got_cross,
     states,
     hidden,
+    onehot_ref,
+    fout_raw,
     fin_ref,
     fout_ref,
     scaled,
@@ -57,6 +59,7 @@
     pop_send,
     pop_recv,
     self_sem,
+    load_sem,
 ):
     pop, chunks, group, steps, member_rows, seqs, rank, width, full, coef = dims
     parts = pair_send.shape[2]
@@ -96,9 +99,10 @@
             weight_sem.at[layer, slot],
         )
 
-    for layer in range(2):
-        for slot in range(4):
-            weight_copy(layer, slot).start()
+    for slot in range(4):
+        weight_copy(0, slot).start()
+    fout_load = pltpu.make_async_copy(fout_hbm, fout_raw, load_sem)
+    fout_load.start()
 
     barrier = pltpu.get_barrier_semaphore()
     for other in others:
@@ -277,16 +281,21 @@
                 read(), weights[layer, slot, :, halves[p]], preferred_element_type=f32
             ).astype(bf16)
 
+        def summed(p):
+            value = product(1, p).astype(f32)
+            pair_copy(k, 0, p).wait_recv()
+            own_cross[k, p, :count] = (value + got_pair[k, 0, p, :count].astype(f32)).astype(bf16)
+            cross_copy(k, p).start()
+
         before(0)
         for p in range(parts):
             own_pair[k, 0, p, :count] = product(0, p)
             pair_copy(k, 0, p).start()
-        before(1)
-        for p in range(parts):
-            value = product(1, p).astype(f32)
-            pair_copy(k, 0, p).wait_recv()
-            own_cross[k, p, :count] = (value + got_pair[k, 0, p, :count].astype(f32)).astype(bf16)
-            cross_copy(k, p).start()
+            if p == 1:
+                before(1)
+            if p:
+                summed(p - 1)
+        summed(parts - 1)
         before(2)
         for p in range(parts):
             own_pair[k, 1, p, :count] = product(2, p)
@@ -380,10 +389,21 @@
         lambda slot: weight_copy(0, slot).wait(),
         put_first,
     )
+    for slot in range(4):
+        weight_copy(1, slot).start()
+    fout_load.wait()
     lax.fori_loop(0, chunks, unpack, 0)
     send_with(out_copy)
 
     def begin(g, carry):
+        tokens = jnp.concatenate(
+            [ids_ref[g * member_rows + m] for m in range(member_rows)], axis=0
+        )
+        entries = lax.broadcasted_iota(jnp.int32, (group, vocab), 1)
+        for t in range(steps):
+            onehot_ref[g, t * group : (t + 1) * group, :] = jnp.where(
+                tokens[:, t : t + 1] == entries, 1.0, 0.0
+            ).astype(bf16)
         features = jnp.dot(onehot_ref[g], embed_ref[...], preferred_element_type=f32).astype(bf16)
         hidden[g] = features
         low_start(0, g, features)
@@ -444,8 +464,9 @@
 
     def finish(g, carry):
         last = normed(1, g)
-        at = pl.ds(pl.multiple_of(g * group, group), group)
-        final_ref[at, :] = last[rows - group :]
+        ending = last[rows - group :].astype(f32)
+        for m in range(member_rows):
+            final_ref[g * member_rows + m] = ending[m * seqs : (m + 1) * seqs].astype(bf16)
         total = last[:group].astype(f32)
         for t in range(1, steps):
             total = total + last[t * group : (t + 1) * group].astype(f32)
@@ -460,18 +481,24 @@
 
     lax.fori_loop(0, chunks, lambda g, carry: finish(g, layer_one(g, carry)), 0)
 
-    def collect(g, carry):
+    lane = lax.broadcasted_iota(jnp.int32, (seqs, lanes), 1)
+
+    def collect(g, scores):
         for r in range(3):
             mark_copy(g, r).wait_recv()
-        at = pl.ds(pl.multiple_of(g * group, group), group)
-        score_ref[at, :] = (marks[g, 0] + marks[g, 1]) + (marks[g, 2] + marks[g, 3])
+        total = (marks[g, 0] + marks[g, 1]) + (marks[g, 2] + marks[g, 3])
+        total = jnp.sum(total, axis=1, keepdims=True) * (full ** (-0.5) / steps)
+        for m in range(member_rows):
+            scores = jnp.where(
+                lane == g * member_rows + m, total[m * seqs : (m + 1) * seqs], scores
+            )
         for r in range(3):
             mark_copy(g, r).wait_send()
             for kind in range(4):
                 small_copy(kind, g, r).wait_send()
-        return carry
-
-    lax.fori_loop(0, chunks, collect, 0)
+        return scores
+
+    score_ref[...] = lax.fori_loop(0, chunks, collect, jnp.zeros((seqs, lanes), f32))
 
     def drain(k, carry):
         for p in range(parts):
@@ -519,9 +546,6 @@
     group = member_rows * seqs
     rows = group * steps
     local = members * rank
-    ids = token_ids.reshape(chunks, member_rows, seqs, steps)
-    ids = jnp.transpose(ids, (0, 3, 1, 2)).reshape(chunks, rows)
-    onehot = (ids[:, :, None] == jnp.arange(vocab, dtype=jnp.int32)).astype(bf16)
     dims = (pop, chunks, group, steps, member_rows, seqs, rank, width, full, coef)
     vmem = pl.BlockSpec(memory_space=pltpu.VMEM)
     smem = pl.BlockSpec(memory_space=pltpu.SMEM)
@@ -530,15 +554,15 @@
     phases = chunks + 1
     parts = 4
     dma = pltpu.SemaphoreType.DMA
-    final, marks, gin, gout = pl.pallas_call(
+    final_features, marks, gin, gout = pl.pallas_call(
         functools.partial(policy_kernel, dims),
         out_shape=(
-            jax.ShapeDtypeStruct((members * seqs, width), bf16),
-            jax.ShapeDtypeStruct((members * seqs, lanes), f32),
+            jax.ShapeDtypeStruct((members, seqs, width), bf16),
+            jax.ShapeDtypeStruct((seqs, lanes), f32),
             jax.ShapeDtypeStruct((layers, pop * local, width), bf16),
             jax.ShapeDtypeStruct((layers, pop * local, columns), bf16),
         ),
-        in_specs=[vmem, vmem, hbm, vmem, vmem, smem, vmem, vmem, vmem],
+        in_specs=[vmem, vmem, hbm, vmem, hbm, smem, vmem, vmem, vmem],
         out_specs=(vmem, vmem, hbm, hbm),
         scratch_shapes=[
             pltpu.VMEM((layers, 4, width, width), bf16),
@@ -548,6 +572,8 @@
             pltpu.VMEM((phases, parts, most, width // parts), bf16),
             pltpu.VMEM((chunks, most, width), f32),
             pltpu.VMEM((chunks, rows, width), bf16),
+            pltpu.VMEM((chunks, rows, vocab), bf16),
+            pltpu.VMEM((layers, members, rank, full), bf16),
             pltpu.VMEM((layers, local, width), bf16),
             pltpu.VMEM((layers, local, full), bf16),
             pltpu.VMEM((layers, local, width), bf16),
@@ -569,12 +595,13 @@
             dma((3, pop)),
             dma((3, pop)),
             dma((2,)),
+            dma,
         ],
         compiler_params=pltpu.CompilerParams(
             collective_id=0, has_side_effects=True, vmem_limit_bytes=60 * 1024 * 1024
         ),
     )(
-        onehot,
+        token_ids,
         embedding,
         mix_weights,
         factors_in,
@@ -584,8 +611,7 @@
         norm_gain,
         reward_dir.reshape(1, width),
     )
-    final_features = final.reshape(members, seqs, width)
-    scores = jnp.sum(marks, axis=1).reshape(members, seqs) * (full ** (-0.5) / steps)
+    scores = marks[:, :members].T
     weight_delta = jnp.einsum("lki,lko->lio", gin, gout, preferred_element_type=f32)
     weight_step = weight_delta * (members_all * rank) ** (-0.5)
     return (final_features, scores, weight_step)

time: 93.2 us -> 88.9 us (0.954)
  other arithmetic: 1.77 us -> 0 us
  local copies, waits for them, and re-layouts: 3.36 us -> 1.93 us
    reshape x2 -> x0, local copies, waits for them, and re-layouts: 2.46 us -> none  [the longest x1 1.58 us: shards(): final_features = final.reshape(members, seqs, width)]
    transpose x0 -> x1, local copies, waits for them, and re-layouts: none -> 1.28 us  [shards(): scores = marks[:, :members].T]
    pallas_call x1, Pallas kernels: 82.1 us -> 81.2 us  [shards(): pl.pallas_call(functools.partial(policy_kernel, dims), out_shape=(jax.Sha...]
where the time goes in v4:
time: 88.9 us; the launch traced here: 88.7 us
  Pallas kernels  81.2 us (91%)
  matrix products  4.91 us (6%)
  local copies, waits for them, and re-layouts  1.93 us (2%)
    pallas_call x1, Pallas kernels, shards(): pl.pallas_call(functools.partial(policy_kernel, dims), out_shape=(jax.Sha...  81.2 us
    dot_general x1, matrix products, shards(): jnp.einsum('lki,lko->lio', gin, gout, preferred_element_type=f32)  4.91 us

profile of v4, /device:TPU:0, one launch (start us, length us, event | category | flops | bytes accessed | tf_op | source)
XLA Modules:
  0.0 88.7 jit_solution(15229965297545629802)
XLA Ops:
  0.6 81.2 %shard_map.112 = (bf16[12,4,1024]{2,1,0:T(4,128)(2,1)}, f32[4,128]{1,0:T(4,128)}, bf16[2,384,1024]{2,1,0:T(8,128)(2,1)}, bf16[2,384,512]{2,1,0:T(8,128)(2,1)}) custom-call(s32[12,4,16]{2,1,0:T(4,128)} %ids_ref.1, bf16[256,1024]{1,0:T(8,128)(2,1)} %embed_ref.1, bf16[2,1024,4096]{2,1,0:T(8,128)(2,1)} %mix_ref.1, bf16[2,12,4,1024]{3,2,1,0:T(4,128)(2,1)} %fin_raw.1, ...), custom_call_target="tpu_custom_call" | custom-call | tf_op jit(solution)/shard_map/pallas_call | solution.py:557
  81.8 0.0 copy-start
  81.8 1.3 %slice_bitcast_fusion = f32[12,4]{0,1:T(4,128)} fusion(f32[4,128]{1,0:T(4,128)} %get-tuple-element.8), kind=kLoop, calls=%fused_computation.1 | loop fusion | bytes 384 | tf_op jit(solution)/shard_map/transpose | solution.py:614
  83.1 4.9 %convolution_multiply_fusion = f32[2,1024,512]{2,1,0:T(8,128)} fusion(bf16[2,384,1024]{2,1,0:T(8,128)(2,1)} %get-tuple-element.9, bf16[2,384,512]{2,1,0:T(8,128)(2,1)} %get-tuple-element.10), kind=kOutput, calls=%fused_computation | convolution fusion | flops 806354944 | bytes 6553600 | tf_op jit(solution)/shard_map/lki,lko->lio/dot_general | solution.py:615
  88.0 0.0 copy-done
  88.0 0.6 copy.15
Async XLA Ops:
  81.8 6.2 %copy-start = (bf16[12,4,1024]{2,1,0:T(4,128)(2,1)S(1)}, bf16[12,4,1024]{2,1,0:T(4,128)(2,1)}, u32[]{:S(2)}) copy-start(bf16[12,4,1024]{2,1,0:T(4,128)(2,1)} %get-tuple-element.14) | copy-start | bytes 294916
